TPU v7x, 32 devices: a whole 2x2x4 slice. The times are simulated.
32 devices in a mesh: dp: 2 (over x), tp: 4 (over z), ep: 4 (over y, core).
Axes of the slice: x: 2, y: 2, z: 4, core: 2. Of those that a mesh axis runs over, the one named last changes fastest.
Arguments:
- tokens: bfloat16 [2048, 768], P(('dp', 'ep')), parts along dimension 0
- grad_out: bfloat16 [2048, 768], P(('dp', 'ep')), parts along dimension 0
- w_router: bfloat16 [768, 16], replicated
- w_in: bfloat16 [16, 768, 3072], P('ep', None, 'tp')
- w_out: bfloat16 [16, 3072, 768], P('ep', 'tp')
- expert_ids: int32 [2048], P(('dp', 'ep')), parts along dimension 0
Outputs:
- output 1: bfloat16 [2048, 768], P(('dp', 'ep')), parts along dimension 0
- output 2: bfloat16 [2048, 768], P(('dp', 'ep')), parts along dimension 0
- output 3: float32 [32, 768, 3072], P(('dp', 'ep'), None, 'tp'), parts along dimension 0
- output 4: float32 [32, 3072, 768], P(('dp', 'ep'), 'tp'), parts along dimension 0
- output 5: float32 [1536, 16], P('dp'), parts along dimension 0
There are 2 independent parts. A program takes and returns all parts, laid end to end along the dimension named above; an argument that names none is the same for every part.
All inputs are finite; a program needn't handle non-finite values.
Results may differ from a plain program's by a relative error of at most 0.00644388.
Values are sent between devices in bfloat16 or wider.
A program may use at most 1 GiB of HBM per device.

v0:
```python
import jax
import jax.numpy as jnp
from jax import lax
from jax.sharding import PartitionSpec as P


def solution(mesh):
    ep_size = mesh.shape["ep"]
    row_spec = P(("dp", "ep"), None)

    def local_block(tokens, grad_out, w_router, w_in, w_out, expert_ids):
        n_local, d_model = tokens.shape
        n_experts = w_router.shape[1]
        local_experts = w_in.shape[0]
        capacity = (6 * n_local + 5 * n_experts - 1) // (5 * n_experts)
        n_slots = n_experts * capacity
        chosen = expert_ids[:, None] == jnp.arange(n_experts)[None, :]
        one_hot = chosen.astype(jnp.int32)
        position = jnp.sum(jnp.cumsum(one_hot, axis=0) * one_hot, axis=1) - 1
        slot_index = jnp.where(position < capacity, expert_ids * capacity + position, n_slots)

        def dispatch(rows):
            slot_buf = jnp.zeros((n_slots + 1, d_model), rows.dtype).at[slot_index].set(rows)
            send_buf = slot_buf[:n_slots].reshape(ep_size, local_experts, capacity, d_model)
            recv_buf = lax.all_to_all(send_buf, "ep", 0, 2, tiled=True)
            return recv_buf.reshape(local_experts, ep_size * capacity, d_model)

        def combine(expert_rows):
            send_buf = expert_rows.reshape(local_experts, ep_size, capacity, d_model)
            recv_buf = lax.all_to_all(send_buf, "ep", 1, 0, tiled=True)
            padded = jnp.concatenate([recv_buf.reshape(n_slots, d_model), jnp.zeros((1, d_model), expert_rows.dtype)], axis=0)
            return jnp.take(padded, slot_index, axis=0)

        logits = jnp.dot(tokens, w_router, preferred_element_type=jnp.float32)
        router_prob = jax.nn.softmax(logits, axis=-1)
        gate_prob = jnp.sum(jnp.where(chosen, router_prob, 0.0), axis=1)

        slot_rows = dispatch(tokens)
        pre_act = jnp.einsum("erd,edf->erf", slot_rows, w_in, preferred_element_type=jnp.float32)
        act_val, act_vjp = jax.vjp(jax.nn.gelu, pre_act)
        hidden = act_val.astype(jnp.bfloat16)
        y_part = jnp.einsum("erf,efd->erd", hidden, w_out, preferred_element_type=jnp.float32)
        y_rows = lax.psum(y_part, "tp").astype(jnp.bfloat16)
        y_tok = combine(y_rows)
        moe_out = (gate_prob[:, None] * y_tok.astype(jnp.float32)).astype(jnp.bfloat16)

        dy_tok = (gate_prob[:, None] * grad_out.astype(jnp.float32)).astype(jnp.bfloat16)
        dy_rows = dispatch(dy_tok)
        d_hidden = jnp.einsum("erd,efd->erf", dy_rows, w_out, preferred_element_type=jnp.float32)
        d_pre = act_vjp(d_hidden)[0].astype(jnp.bfloat16)
        grad_w_out = jnp.einsum("erf,erd->efd", hidden, dy_rows, preferred_element_type=jnp.float32)
        grad_w_in = jnp.einsum("erd,erf->edf", slot_rows, d_pre, preferred_element_type=jnp.float32)
        d_part = jnp.einsum("erf,edf->erd", d_pre, w_in, preferred_element_type=jnp.float32)
        d_slot = lax.psum(d_part, "tp").astype(jnp.bfloat16)
        dx_moe = combine(d_slot)

        d_gate = jnp.sum(grad_out.astype(jnp.float32) * y_tok.astype(jnp.float32), axis=1)
        d_logits = (d_gate[:, None] * router_prob * (chosen.astype(jnp.float32) - gate_prob[:, None])).astype(jnp.bfloat16)
        router_grad = jnp.einsum("te,de->td", d_logits, w_router, preferred_element_type=jnp.float32)
        grad_tokens = (dx_moe.astype(jnp.float32) + router_grad).astype(jnp.bfloat16)
        grad_w_router = lax.psum(jnp.einsum("td,te->de", tokens, d_logits, preferred_element_type=jnp.float32), "ep")
        return moe_out, grad_tokens, grad_w_in, grad_w_out, grad_w_router

    in_specs = (row_spec, row_spec, P(None, None), P("ep", None, "tp"), P("ep", "tp", None), P(("dp", "ep")))
    out_specs = (row_spec, row_spec, P(("dp", "ep"), None, "tp"), P(("dp", "ep"), "tp", None), P("dp", None))
    return jax.shard_map(local_block, mesh=mesh, in_specs=in_specs, out_specs=out_specs, check_vma=False)
```

profile of v0, /device:TPU:0, one launch (start us, length us, event | category | flops | bytes accessed | tf_op | source)
XLA Modules:
  0.0 150.8 jit_solution(15633268213121134764)
XLA Ops:
  0.7 0.8 fusion.29
  1.4 0.6 reduce-window.6
  2.0 0.2 slice_reduce_fusion
  2.2 0.8 fusion.28
  3.0 0.7 compare_and_fusion
  3.7 2.2 %scatter_custom_fusion = bf16[321,768]{1,0:T(8,128)(2,1)S(1)} fusion(s32[256]{0:T(256)S(1)} %get-tuple-element.9, bf16[256,768]{1,0:T(8,128)(2,1)} %param.8, bf16[]{:T(256)} %constant.6.clone.1), kind=kCustom, calls=%fused_computation.35 | custom fusion | bytes 493568 | tf_op jit(solution)/shard_map/scatter | solution.py:23
  6.1 1.0 copy.26
  7.0 4.3 %all-to-all-start = ((bf16[4,4,20,768]{3,1,2,0:T(4,128)(2,1)}), bf16[4,4,20,768]{3,1,2,0:T(4,128)(2,1)S(1)}, u32[]{:S(2)}, u32[]{:S(2)}) async-start(bf16[4,4,20,768]{3,1,2,0:T(4,128)(2,1)} %copy.26), calls=%async_computation | async-start | bytes 983040 | tf_op jit(solution)/shard_map/all_to_all | solution.py:25
  11.3 0.3 fusion.33
  11.7 1.8 %scatter_custom_fusion.1 = bf16[321,768]{1,0:T(8,128)(2,1)S(1)} fusion(s32[256]{0:T(256)S(1)} %get-tuple-element.9, bf16[256,768]{1,0:T(8,128)(2,1)S(1)} %copy-done.3, f32[256]{0:T(256)S(1)} %select_reduce_fusion, bf16[]{:T(256)} %constant.6.clone.1), kind=kCustom, calls=%fused_computation.31 | custom fusion | flops 589824 | bytes 887298 | tf_op jit(solution)/shard_map/scatter | solution.py:23
  13.7 1.0 copy.30
  14.6 4.9 %all-to-all-done = bf16[4,4,20,768]{3,1,2,0:T(4,128)(2,1)S(1)} async-done(((bf16[4,4,20,768]{3,1,2,0:T(4,128)(2,1)}), bf16[4,4,20,768]{3,1,2,0:T(4,128)(2,1)S(1)}, u32[]{:S(2)}, u32[]{:S(2)}) %all-to-all-start) | async-done | bytes 491552 | tf_op jit(solution)/shard_map/all_to_all | solution.py:25
  19.6 3.5 %all-to-all-start.2 = ((bf16[4,4,20,768]{3,1,2,0:T(4,128)(2,1)}), bf16[4,4,20,768]{3,1,2,0:T(4,128)(2,1)S(1)}, u32[]{:S(2)}, u32[]{:S(2)}) async-start(bf16[4,4,20,768]{3,1,2,0:T(4,128)(2,1)} %copy.30), calls=%async_computation.2 | async-start | bytes 983040 | tf_op jit(solution)/shard_map/all_to_all | solution.py:25
  23.1 3.4 %fusion.19 = f32[4,80,768]{2,1,0:T(8,128)S(1)} fusion(bf16[4,768,768]{2,1,0:T(8,128)(2,1)} %param.11, bf16[4,80,768]{2,0,1:T(4,128)(2,1)S(1)} %bitcast.54), kind=kOutput, calls=%fused_computation.29 | convolution fusion | flops 377487360 | bytes 6193152 | tf_op jit(solution)/shard_map/erd,edf->erf/dot_general | solution.py:39
  26.4 0.2 slice-done.2
  26.8 1.0 fusion.32
  27.8 3.5 %all-to-all-done.2 = bf16[4,4,20,768]{3,1,2,0:T(4,128)(2,1)S(1)} async-done(((bf16[4,4,20,768]{3,1,2,0:T(4,128)(2,1)}), bf16[4,4,20,768]{3,1,2,0:T(4,128)(2,1)S(1)}, u32[]{:S(2)}, u32[]{:S(2)}) %all-to-all-start.2) | async-done | bytes 491552 | tf_op jit(solution)/shard_map/all_to_all | solution.py:25
  31.3 4.1 %fusion.7 = bf16[4,80,768]{2,1,0:T(8,128)(2,1)S(1)} fusion(f32[4,80,768]{2,1,0:T(8,128)S(1)} %fusion.19, bf16[4,768,768]{2,1,0:T(8,128)(2,1)} %param.12, bf16[4,80,768]{2,0,1:T(4,128)(2,1)S(1)} %bitcast.58), kind=kOutput, calls=%fused_computation.15 | convolution fusion | flops 382402560 | bytes 6684672 | tf_op jit(solution)/shard_map/erd,efd->erf/dot_general | solution.py:49
  35.4 5.2 %fusion.11 = f32[4,768,768]{2,1,0:T(8,128)} fusion(bf16[4,80,768]{2,0,1:T(4,128)(2,1)S(1)} %bitcast.59, f32[4,80,768]{2,1,0:T(8,128)S(1)} %fusion.19), kind=kOutput, calls=%fused_computation.23 | convolution fusion | flops 379699200 | bytes 10911744 | tf_op jit(solution)/shard_map/erf,erd->efd/dot_general | solution.py:51
  40.6 1.5 %fusion.34 = f32[4,80,768]{2,1,0:T(8,128)S(1)} fusion(bf16[4,80,768]{2,1,0:T(8,128)(2,1)S(1)} %fusion.7, bf16[4,768,768]{2,1,0:T(8,128)(2,1)S(1)} %bitcast.53), kind=kOutput, calls=%fused_computation.56 | convolution fusion | flops 377487360 | bytes 6193152 | tf_op jit(solution)/shard_map/erf,edf->erd/dot_general | solution.py:53
  42.1 73.6 %all-reduce.4 = (bf16[4,80,768]{2,1,0:T(8,128)(2,1)}, bf16[4,80,768]{2,1,0:T(8,128)(2,1)S(1)}) all-reduce(f32[4,80,768]{2,1,0:T(8,128)S(1)} %fusion.32, f32[4,80,768]{2,1,0:T(8,128)S(1)} %fusion.34), channel_id=1, replica_groups=mesh['dp'=2,'tp'=4,'ep'=4] {'tp'}, use_global_device_ids=true, to_apply=%region_7.8 | all-reduce | flops 491520 | bytes 2949120 | tf_op jit(solution)/shard_map/psum | solution.py:43
  115.7 2.1 %copy.28 = bf16[4,80,768]{2,0,1:T(4,128)(2,1)} copy(bf16[4,80,768]{2,1,0:T(8,128)(2,1)} %get-tuple-element.6) | data formatting | bytes 983040 | tf_op jit(solution)/shard_map/convert_element_type | solution.py:43
  117.7 3.5 %all-to-all-start.1 = ((bf16[4,4,20,768]{3,0,2,1:T(4,128)(2,1)}), bf16[4,4,20,768]{3,0,2,1:T(4,128)(2,1)S(1)}, u32[]{:S(2)}, u32[]{:S(2)}) async-start(bf16[4,4,20,768]{3,0,2,1:T(4,128)(2,1)} %bitcast.5), calls=%async_computation.1 | async-start | bytes 983040 | tf_op jit(solution)/shard_map/all_to_all | solution.py:30
  121.2 1.0 copy.32
  122.2 5.2 %fusion.17 = f32[4,768,768]{2,1,0:T(8,128)} fusion(bf16[4,80,768]{2,1,0:T(8,128)(2,1)S(1)} %fusion.7, bf16[4,80,768]{2,0,1:T(4,128)(2,1)S(1)} %bitcast.55), kind=kOutput, calls=%fused_computation.27 | convolution fusion | flops 377487360 | bytes 10420224 | tf_op jit(solution)/shard_map/erd,erf->edf/dot_general | solution.py:52
  127.4 2.0 %all-to-all-done.1 = bf16[4,4,20,768]{3,0,2,1:T(4,128)(2,1)S(1)} async-done(((bf16[4,4,20,768]{3,0,2,1:T(4,128)(2,1)}), bf16[4,4,20,768]{3,0,2,1:T(4,128)(2,1)S(1)}, u32[]{:S(2)}, u32[]{:S(2)}) %all-to-all-start.1) | async-done | bytes 491552 | tf_op jit(solution)/shard_map/all_to_all | solution.py:30
  129.4 3.6 %all-to-all-start.3 = ((bf16[4,4,20,768]{3,0,2,1:T(4,128)(2,1)}), bf16[4,4,20,768]{3,0,2,1:T(4,128)(2,1)S(1)}, u32[]{:S(2)}, u32[]{:S(2)}) async-start(bf16[4,4,20,768]{3,0,2,1:T(4,128)(2,1)} %bitcast.11), calls=%async_computation.3 | async-start | bytes 983040 | tf_op jit(solution)/shard_map/all_to_all | solution.py:30
  133.3 1.2 gather_fusion
  134.5 1.1 fusion.10
  135.8 12.5 %psum.23 = f32[768,16]{0,1:T(8,128)} all-reduce(f32[768,16]{0,1:T(8,128)S(1)} %convolution_bitcast_fusion), channel_id=1, replica_groups=mesh['dp'=2,'tp'=4,'ep'=4] {'ep'}, use_global_device_ids=true, to_apply=%region_11.13 | all-reduce | flops 12288 | bytes 98304 | tf_op jit(solution)/shard_map/psum | solution.py:61
  148.5 1.2 gather_fusion.1
  149.7 1.1 fusion
  (38 shorter events, 1.1 us)
Async XLA Ops:
  0.6 10.7 %copy-start = (bf16[768,16]{0,1:T(8,128)(2,1)S(1)}, bf16[768,16]{0,1:T(8,128)(2,1)}, u32[]{:S(2)}) copy-start(bf16[768,16]{0,1:T(8,128)(2,1)} %param.10) | copy-start | bytes 73732
  0.6 11.0 %copy-start.5 = (s32[256]{0:T(256)S(1)}, s32[256]{0:T(256)}, u32[]{:S(2)}) copy-start(s32[256]{0:T(256)} %param.13) | copy-start | bytes 3076
  0.7 10.7 %copy-start.1 = (bf16[256,768]{1,0:T(8,128)(2,1)S(1)}, bf16[256,768]{1,0:T(8,128)(2,1)}, u32[]{:S(2)}) copy-start(bf16[256,768]{1,0:T(8,128)(2,1)} %param.8) | copy-start | bytes 1179652
  0.7 11.0 %copy-start.3 = (bf16[256,768]{1,0:T(8,128)(2,1)S(1)}, bf16[256,768]{1,0:T(8,128)(2,1)}, u32[]{:S(2)}) copy-start(bf16[256,768]{1,0:T(8,128)(2,1)} %param.9) | copy-start | bytes 1179652
  7.0 12.6 %all-to-all-start = ((bf16[4,4,20,768]{3,1,2,0:T(4,128)(2,1)}), bf16[4,4,20,768]{3,1,2,0:T(4,128)(2,1)S(1)}, u32[]{:S(2)}, u32[]{:S(2)}) async-start(bf16[4,4,20,768]{3,1,2,0:T(4,128)(2,1)} %copy.26), calls=%async_computation | async-start | bytes 983040 | tf_op jit(solution)/shard_map/all_to_all | solution.py:25
  19.6 11.7 %all-to-all-start.2 = ((bf16[4,4,20,768]{3,1,2,0:T(4,128)(2,1)}), bf16[4,4,20,768]{3,1,2,0:T(4,128)(2,1)S(1)}, u32[]{:S(2)}, u32[]{:S(2)}) async-start(bf16[4,4,20,768]{3,1,2,0:T(4,128)(2,1)} %copy.30), calls=%async_computation.2 | async-start | bytes 983040 | tf_op jit(solution)/shard_map/all_to_all | solution.py:25
  23.1 3.6 %slice-start.2 = ((s8[4718592]{0:T(1024)(128)(4,1)}), s8[4194304]{0:T(1024)(128)(4,1)S(1)}, s32[]{:S(2)}) async-start(s8[4718592]{0:T(1024)(128)(4,1)} %bitcast.56), calls=%async_computation.6 | async-start | bytes 8388608
  23.1 3.7 %slice-start.3 = ((s8[4718592]{0:T(1024)(128)(4,1)}), s8[524288]{0:T(1024)(128)(4,1)S(1)}, s32[]{:S(2)}) async-start(s8[4718592]{0:T(1024)(128)(4,1)} %bitcast.56), calls=%async_computation.7 | async-start | bytes 1048576
  31.3 9.3 %slice-start = ((s8[4718592]{0:T(1024)(128)(4,1)}), s8[524288]{0:T(1024)(128)(4,1)S(1)}, s32[]{:S(2)}) async-start(s8[4718592]{0:T(1024)(128)(4,1)} %bitcast.52), calls=%async_computation.4 | async-start | bytes 1048576
  35.4 5.2 %slice-start.1 = ((s8[4718592]{0:T(1024)(128)(4,1)}), s8[4194304]{0:T(1024)(128)(4,1)S(1)}, s32[]{:S(2)}) async-start(s8[4718592]{0:T(1024)(128)(4,1)} %bitcast.52), calls=%async_computation.5 | async-start | bytes 8388608
  117.7 11.7 %all-to-all-start.1 = ((bf16[4,4,20,768]{3,0,2,1:T(4,128)(2,1)}), bf16[4,4,20,768]{3,0,2,1:T(4,128)(2,1)S(1)}, u32[]{:S(2)}, u32[]{:S(2)}) async-start(bf16[4,4,20,768]{3,0,2,1:T(4,128)(2,1)} %bitcast.5), calls=%async_computation.1 | async-start | bytes 983040 | tf_op jit(solution)/shard_map/all_to_all | solution.py:30
  127.4 7.1 %copy-start.4 = (bf16[256,768]{1,0:T(8,128)(2,1)S(1)}, bf16[256,768]{1,0:T(8,128)(2,1)}, u32[]{:S(2)}) copy-start(bf16[256,768]{1,0:T(8,128)(2,1)} %param.9) | copy-start | bytes 1179652
  127.4 8.2 %copy-start.2 = (bf16[256,768]{1,0:T(8,128)(2,1)S(1)}, bf16[256,768]{1,0:T(8,128)(2,1)}, u32[]{:S(2)}) copy-start(bf16[256,768]{1,0:T(8,128)(2,1)} %param.8) | copy-start | bytes 1179652
  129.4 18.9 %all-to-all-start.3 = ((bf16[4,4,20,768]{3,0,2,1:T(4,128)(2,1)}), bf16[4,4,20,768]{3,0,2,1:T(4,128)(2,1)S(1)}, u32[]{:S(2)}, u32[]{:S(2)}) async-start(bf16[4,4,20,768]{3,0,2,1:T(4,128)(2,1)} %bitcast.11), calls=%async_computation.3 | async-start | bytes 983040 | tf_op jit(solution)/shard_map/all_to_all | solution.py:30
where the time goes:
time: 151 us
  blocking collectives  86.1 us (57%)
  matrix products  21.8 us (14%)
  starting transfers between devices  14.9 us (10%)
  local copies, waits for them, and re-layouts  10.9 us (7%)
  waiting for transfers between devices  10.5 us (7%)
  other arithmetic  5.82 us (4%)
    psum x1, blocking collectives, local_block(): y_rows = lax.psum(y_part, 'tp').astype(jnp.bfloat16)  73.6 us
    psum x1, blocking collectives, local_block(): lax.psum(jnp.einsum('td,te->de', tokens, d_logits, preferred_element_type...  12.5 us
    all_to_all x2, waiting for transfers between devices, dispatch(): recv_buf = lax.all_to_all(send_buf, 'ep', 0, 2, tiled=True)  8.47 us
    all_to_all x2, starting transfers between devices, dispatch(): recv_buf = lax.all_to_all(send_buf, 'ep', 0, 2, tiled=True)  7.77 us
    all_to_all x2, starting transfers between devices, combine(): recv_buf = lax.all_to_all(send_buf, 'ep', 1, 0, tiled=True)  7.12 us
    dot_general x1, matrix products, local_block(): jnp.einsum('erf,erd->efd', hidden, dy_rows, preferred_element_type=jnp.fl...  5.2 us
    dot_general x1, matrix products, local_block(): jnp.einsum('erd,erf->edf', slot_rows, d_pre, preferred_element_type=jnp.f...  5.18 us
    dot_general x1, matrix products, local_block(): jnp.einsum('erd,efd->erf', dy_rows, w_out, preferred_element_type=jnp.flo...  4.08 us
  transfers between devices with their start and end apart: 4, of which 3 were waited for; matrix products, arithmetic and copies ran while one was open for 11% of the time, Pallas kernels for 0%

commit v1 on v0

v1 whole, which is shorter than its diff:
```python
import functools

import jax
import jax.numpy as jnp
from jax import lax
from jax.experimental import pallas as pl
from jax.experimental.pallas import tpu as pltpu
from jax.sharding import PartitionSpec as P

MESH = pl.DeviceIdType.MESH
F32, BF16 = jnp.float32, jnp.bfloat16
GELU_C = 0.7978845608028654
GELU_K = 0.044715
N_EP, N_TP, N_PAIR = 4, 4, 2


def dot(a, b, dims=((1,), (0,))):
    return lax.dot_general(a, b, (dims, ((), ())), preferred_element_type=F32)


def pair_masks(rows, block, cap):
    row = lax.broadcasted_iota(jnp.int32, (rows, 1), 0)
    first = lax.rem(row, block) < cap
    return jnp.where(first, 1.0, 0.0).astype(BF16), jnp.where(first, 0.0, 1.0).astype(BF16)


def moe_kernel(
    cap,
    ids_ref, wg_ref, x_hbm, gy_hbm, wi_hbm, wo_hbm,
    out_hbm, dx_hbm, dwg_hbm, h_hbm, da_hbm, xr_hbm, dyr_hbm,
    x_v, gy_v, wi_v, wo_v,
    onehot_slots, router_v, send_v, recv_v, act_v, h_v, da_v,
    part_v, relay_in, relay_out, fin_in, red_v, slots_v,
    out_v, dx_v, dwg_part, dwg_in, dwg_v,
    load_sem, store_sem, disp_send, disp_recv, rs_send, rs_recv, hop_send, hop_recv, ag_send, ag_recv, wg_send, wg_recv,
):
    block = 2 * cap
    rows = N_EP * block
    n_tok, d_model = x_v.shape
    n_exp = wg_ref.shape[1]
    half = d_model // 2
    z, j = lax.axis_index("tp"), lax.axis_index("ep")
    right, left, far = lax.rem(z + 1, N_TP), lax.rem(z + 3, N_TP), lax.rem(z + 2, N_TP)
    ep_peer = [lax.rem(j + k, N_EP) for k in range(N_EP)]

    def remote(src, dst, ssem, rsem, **dev):
        return pltpu.make_async_remote_copy(
            src_ref=src, dst_ref=dst, send_sem=ssem, recv_sem=rsem, device_id=dev, device_id_type=MESH
        )

    load_x = pltpu.make_async_copy(x_hbm, x_v, load_sem.at[0])
    load_gy = pltpu.make_async_copy(gy_hbm, gy_v, load_sem.at[1])
    load_wi = [pltpu.make_async_copy(wi_hbm.at[pl.ds(2 * p, 2)], wi_v.at[pl.ds(2 * p, 2)], load_sem.at[2 + p]) for p in range(2)]
    load_wo = [pltpu.make_async_copy(wo_hbm.at[pl.ds(2 * p, 2)], wo_v.at[pl.ds(2 * p, 2)], load_sem.at[4 + p]) for p in range(2)]
    load_x.start()
    load_gy.start()
    for p in range(2):
        load_wi[p].start()
        load_wo[p].start()

    barrier = pltpu.get_barrier_semaphore()
    for dev in [{"tp": right}, {"tp": left}] + [{"ep": ep_peer[k]} for k in range(1, N_EP)]:
        pl.semaphore_signal(barrier, inc=1, device_id=dev, device_id_type=MESH)

    ids = ids_ref[...]
    chosen = ids == lax.broadcasted_iota(jnp.int32, (n_exp, n_tok), 0)
    onehot = jnp.where(chosen, 1.0, 0.0)
    before = lax.broadcasted_iota(jnp.int32, (n_tok, n_tok), 0) < lax.broadcasted_iota(jnp.int32, (n_tok, n_tok), 1)
    counts = dot(onehot.astype(BF16), jnp.where(before, 1.0, 0.0).astype(BF16))
    pos = jnp.sum(counts * onehot, axis=0, keepdims=True)
    base = ((ids >> 1) & 1) * rows + (ids >> 2) * block + (ids & 1) * cap
    slot = jnp.where(pos < cap, base.astype(F32) + pos, -1.0)
    slot_iota = lax.broadcasted_iota(jnp.int32, (2 * rows, n_tok), 0).astype(F32)
    onehot_slots[...] = jnp.where(slot_iota == slot, 1.0, 0.0).astype(BF16)

    pl.semaphore_wait(barrier, 5)

    def dispatch(t, tok_rows):
        packed = dot(onehot_slots[...], tok_rows).astype(BF16)
        send_v[t] = packed.reshape(2, N_EP, block, d_model)

    def disp_copy(t, p, k):
        return remote(
            send_v.at[t, p, ep_peer[k]], recv_v.at[t, p, j], disp_send.at[t, p, k - 1], disp_recv.at[t, p, k - 1], ep=ep_peer[k]
        )

    def start_dispatch(t):
        for p in range(N_PAIR):
            for k in (2, 1, 3):
                disp_copy(t, p, k).start()
        for p in range(N_PAIR):
            recv_v[t, p, j] = send_v[t, p, j]

    load_x.wait()
    dispatch(0, x_v[...])
    start_dispatch(0)

    logits = dot(wg_ref[...], x_v[...], ((0,), (1,)))
    expd = jnp.exp(logits - jnp.max(logits, axis=0, keepdims=True))
    prob = expd / jnp.sum(expd, axis=0, keepdims=True)
    gate_row = jnp.sum(jnp.where(chosen, prob, 0.0), axis=0, keepdims=True)
    router_v[...] = prob * (onehot - gate_row)
    gate_col = jnp.transpose(jnp.broadcast_to(gate_row, (128, n_tok)))
    gate_v = gate_col[:, :1]
    load_gy.wait()
    dispatch(1, (gate_v * gy_v[...].astype(F32)).astype(BF16))
    start_dispatch(1)

    mask0, mask1 = pair_masks(rows, block, cap)

    def wait_rows(t, p):
        for k in range(1, N_EP):
            disp_copy(t, p, k).wait_recv()
        return recv_v[t, p].reshape(rows, d_model)

    def pair_dot(lhs, w_ref, p, dims=((1,), (0,))):
        return dot(lhs * mask0, w_ref[2 * p], dims) + dot(lhs * mask1, w_ref[2 * p + 1], dims)

    def blk(zz, p):
        return lax.rem(zz + 2 * p, N_TP)

    def rs_copy(i, p, d, m):
        nxt = right if d == 0 else left
        sem = (rs_send.at[i, d, m], rs_recv.at[i, d, m])
        if m == 0:
            return remote(part_v.at[i, d, blk(far, p)], relay_in.at[i, d], *sem, tp=nxt)
        if m == 1:
            return remote(part_v.at[i, 1 - d, blk(nxt, p)], fin_in.at[i, d, 1 - d], *sem, tp=nxt)
        return remote(relay_out.at[i, d], fin_in.at[i, d, d], *sem, tp=nxt)

    def rs_start(t, p, part):
        i = 2 * t + p
        part_v[i, 0] = part[:, :half].reshape(N_EP, block, half)
        part_v[i, 1] = part[:, half:].reshape(N_EP, block, half)
        for m in (0, 1):
            for d in (0, 1):
                rs_copy(i, p, d, m).start()

    def rs_relay(t, p):
        i = 2 * t + p
        for d in (0, 1):
            rs_copy(i, p, d, 0).wait_recv()
            relay_out[i, d] = relay_in[i, d] + part_v[i, d, blk(right if d == 0 else left, p)]
            rs_copy(i, p, d, 2).start()

    def hop_copy(i, p, k):
        return remote(red_v.at[i], slots_v.at[i, j], hop_send.at[i], hop_recv.at[i, k - 1], ep=ep_peer[k])

    def rs_final(t, p):
        i = 2 * t + p
        for d in (0, 1):
            rs_copy(i, p, d, 1).wait_recv()
            rs_copy(i, p, d, 2).wait_recv()
        mine = blk(z, p)
        whole = [part_v[i, h, mine] + fin_in[i, 0, h] + fin_in[i, 1, h] for h in (0, 1)]
        red_v[i] = jnp.concatenate(whole, axis=1).astype(BF16)
        for k in range(1, N_EP):
            @pl.when(mine == ep_peer[k])
            def _():
                hop_copy(i, p, k).start()

        @pl.when(mine == j)
        def _():
            slots_v[i, j] = red_v[i]

    def ag_copy(i, hlf, n, dev):
        part = slots_v.at[i, pl.ds(2 * hlf, 2)]
        return remote(part, part, ag_send.at[i, n], ag_recv.at[i, hlf], tp=dev)

    def place(p):
        return lax.rem(z + N_TP - blk(j, p) + 0, N_TP)

    def ag_root(t, p):
        i = 2 * t + p

        @pl.when(place(p) == 0)
        def _():
            for k in range(1, N_EP):
                hop_copy(i, p, k).wait_recv()
            ag_copy(i, 0, 0, right).start()
            ag_copy(i, 1, 1, left).start()
            ag_copy(i, 1, 2, right).start()
            ag_copy(i, 0, 3, left).start()

    def ag_forward(t, p):
        i = 2 * t + p

        @pl.when(place(p) == 1)
        def _():
            ag_copy(i, 0, 0, right).wait_recv()
            ag_copy(i, 0, 0, right).start()

        @pl.when(place(p) == 3)
        def _():
            ag_copy(i, 1, 0, left).wait_recv()
            ag_copy(i, 1, 0, left).start()

    def ag_wait(t, p):
        i = 2 * t + p

        @pl.when((place(p) == 1) | (place(p) == 2))
        def _():
            ag_copy(i, 1, 0, right).wait_recv()

        @pl.when((place(p) == 3) | (place(p) == 2))
        def _():
            ag_copy(i, 0, 0, right).wait_recv()

    def forward(p):
        load_wi[p].wait()
        xr = wait_rows(0, p)
        a = pair_dot(xr, wi_v, p)
        act_v[p] = a
        h = (0.5 * a * (1.0 + jnp.tanh(GELU_C * (a + GELU_K * a * a * a)))).astype(BF16)
        h_v[p] = h
        load_wo[p].wait()
        rs_start(0, p, pair_dot(h, wo_v, p))

    def backward(p):
        dyr = wait_rows(1, p)
        dh = pair_dot(dyr, wo_v, p, ((1,), (1,)))
        a = act_v[p]
        a2 = a * a
        th = jnp.tanh(GELU_C * (a + GELU_K * a2 * a))
        slope = 0.5 * (1.0 + th) + 0.5 * a * (1.0 - th * th) * (GELU_C * (1.0 + 3.0 * GELU_K * a2))
        da = (dh * slope).astype(BF16)
        da_v[p] = da
        rs_start(1, p, pair_dot(da, wi_v, p, ((1,), (1,))))

    def combine(t):
        both = jnp.concatenate([slots_v[2 * t + p].reshape(rows, d_model) for p in range(2)], axis=0)
        return dot(onehot_slots[...], both, ((0,), (0,)))

    stores = []

    def store(src, dst):
        cp = pltpu.make_async_copy(src, dst, store_sem.at[len(stores)])
        cp.start()
        stores.append(cp)

    forward(0)
    forward(1)
    rs_relay(0, 0)
    backward(0)
    rs_relay(0, 1)
    rs_final(0, 0)
    backward(1)
    store(h_v, h_hbm)
    store(da_v, da_hbm)
    store(recv_v.at[0], xr_hbm)
    store(recv_v.at[1], dyr_hbm)
    rs_final(0, 1)
    ag_root(0, 0)
    rs_relay(1, 0)
    ag_root(0, 1)
    ag_forward(0, 0)
    rs_relay(1, 1)
    ag_forward(0, 1)
    rs_final(1, 0)
    rs_final(1, 1)
    ag_wait(0, 0)
    ag_wait(0, 1)
    ag_root(1, 0)
    ag_root(1, 1)

    y_tok = combine(0)
    out_v[...] = (gate_v * y_tok).astype(BF16)
    store(out_v, out_hbm)
    d_gate = jnp.sum(gy_v[...].astype(F32) * y_tok, axis=1, keepdims=True)
    d_gate_row = jnp.transpose(jnp.broadcast_to(d_gate, (n_tok, 128)))[:1]
    d_logits = d_gate_row * router_v[...]
    dwg_part[...] = dot(d_logits.astype(BF16), x_v[...])

    def wg_copy(k):
        return remote(dwg_part, dwg_in.at[k - 1], wg_send.at[k - 1], wg_recv.at[k - 1], ep=ep_peer[k])

    for k in range(1, N_EP):
        wg_copy(k).start()
    ag_forward(1, 0)
    router_grad = dot(jnp.transpose(d_logits).astype(BF16), wg_ref[...], ((1,), (1,)))
    ag_forward(1, 1)
    for k in range(1, N_EP):
        wg_copy(k).wait_recv()
    dwg_v[...] = (dwg_part[...] + dwg_in[1]) + (dwg_in[0] + dwg_in[2])
    store(dwg_v, dwg_hbm)
    ag_wait(1, 0)
    ag_wait(1, 1)
    dx_v[...] = (combine(1) + router_grad).astype(BF16)
    store(dx_v, dx_hbm)

    for t in range(2):
        for p in range(N_PAIR):
            i = 2 * t + p
            for k in range(1, N_EP):
                disp_copy(t, p, k).wait_send()
            for d in (0, 1):
                for m in range(3):
                    rs_copy(i, p, d, m).wait_send()

            @pl.when(blk(z, p) != j)
            def _():
                hop_copy(i, p, 1).wait_send()

            @pl.when(place(p) == 0)
            def _():
                for n, hlf in enumerate((0, 1, 1, 0)):
                    ag_copy(i, hlf, n, right).wait_send()

            @pl.when((place(p) == 1) | (place(p) == 3))
            def _():
                ag_copy(i, 0, 0, right).wait_send()
    for k in range(1, N_EP):
        wg_copy(k).wait_send()
    for cp in stores:
        cp.wait()


def grads_kernel(
    cap, h_ref, da_ref, xr_ref, dyr_ref, out_ref, dx_ref, dwg_ref,
    o_out, o_dx, o_wi, o_wo, o_dwg, stage, sem,
):
    block = 2 * cap
    rows = N_EP * block
    d_model = xr_ref.shape[-1]
    o_out[...] = out_ref[...]
    o_dx[...] = dx_ref[...]
    o_dwg[...] = jnp.transpose(dwg_ref[...])
    masks = pair_masks(rows, block, cap)
    copies = []
    for e in range(4):
        p, m = e // 2, masks[e % 2]
        xr = xr_ref[p].reshape(rows, d_model)
        dyr = dyr_ref[p].reshape(rows, d_model)
        stage[2 * e] = dot(h_ref[p] * m, dyr, ((0,), (0,)))
        copies.append(pltpu.make_async_copy(stage.at[2 * e], o_wo.at[e], sem.at[2 * e]))
        copies[-1].start()
        stage[2 * e + 1] = dot(xr * m, da_ref[p], ((0,), (0,)))
        copies.append(pltpu.make_async_copy(stage.at[2 * e + 1], o_wi.at[e], sem.at[2 * e + 1]))
        copies[-1].start()
    for cp in copies:
        cp.wait()


def solution(mesh):
    row_spec = P(("dp", "ep"), None)

    def local_block(tokens, grad_out, w_router, w_in, w_out, expert_ids):
        n_tok, d_model = tokens.shape
        n_exp = w_router.shape[1]
        n_loc, _, f_loc = w_in.shape
        cap = (6 * n_tok + 5 * n_exp - 1) // (5 * n_exp)
        block, rows, half = 2 * cap, 8 * cap, d_model // 2
        S = jax.ShapeDtypeStruct
        any_spec, vmem_spec = pl.BlockSpec(memory_space=pl.ANY), pl.BlockSpec(memory_space=pltpu.VMEM)
        dma = pltpu.SemaphoreType.DMA
        out_shape = (
            S((n_tok, d_model), BF16), S((n_tok, d_model), BF16), S((n_exp, d_model), F32),
            S((2, rows, f_loc), BF16), S((2, rows, f_loc), BF16),
            S((2, N_EP, block, d_model), BF16), S((2, N_EP, block, d_model), BF16),
        )
        scratch = [
            pltpu.VMEM((n_tok, d_model), BF16), pltpu.VMEM((n_tok, d_model), BF16),
            pltpu.VMEM(w_in.shape, BF16), pltpu.VMEM(w_out.shape, BF16),
            pltpu.VMEM((2 * rows, n_tok), BF16), pltpu.VMEM((n_exp, n_tok), F32),
            pltpu.VMEM((2, 2, N_EP, block, d_model), BF16), pltpu.VMEM((2, 2, N_EP, block, d_model), BF16),
            pltpu.VMEM((2, rows, f_loc), F32), pltpu.VMEM((2, rows, f_loc), BF16), pltpu.VMEM((2, rows, f_loc), BF16),
            pltpu.VMEM((4, 2, N_EP, block, half), F32), pltpu.VMEM((4, 2, block, half), F32),
            pltpu.VMEM((4, 2, block, half), F32), pltpu.VMEM((4, 2, 2, block, half), F32),
            pltpu.VMEM((4, block, d_model), BF16), pltpu.VMEM((4, N_EP, block, d_model), BF16),
            pltpu.VMEM((n_tok, d_model), BF16), pltpu.VMEM((n_tok, d_model), BF16),
            pltpu.VMEM((n_exp, d_model), F32), pltpu.VMEM((3, n_exp, d_model), F32), pltpu.VMEM((n_exp, d_model), F32),
            dma((6,)), dma((7,)), dma((2, 2, 3)), dma((2, 2, 3)), dma((4, 2, 3)), dma((4, 2, 3)),
            dma((4,)), dma((4, 3)), dma((4, 4)), dma((4, 2)), dma((3,)), dma((3,)),
        ]
        out, dx, dwg, h, da, xr, dyr = pl.pallas_call(
            functools.partial(moe_kernel, cap),
            out_shape=out_shape,
            in_specs=[vmem_spec, vmem_spec, any_spec, any_spec, any_spec, any_spec],
            out_specs=(any_spec,) * 7,
            scratch_shapes=scratch,
            compiler_params=pltpu.CompilerParams(collective_id=0, has_side_effects=True, vmem_limit_bytes=56 * 2**20),
        )(expert_ids.reshape(1, n_tok), w_router, tokens, grad_out, w_in, w_out)
        out, dx, dwi, dwo, dwg = pl.pallas_call(
            functools.partial(grads_kernel, cap),
            out_shape=(
                S((n_tok, d_model), BF16), S((n_tok, d_model), BF16),
                S((n_loc, d_model, f_loc), F32), S((n_loc, f_loc, d_model), F32), S((d_model, n_exp), F32),
            ),
            in_specs=[vmem_spec] * 7,
            out_specs=(vmem_spec, vmem_spec, any_spec, any_spec, vmem_spec),
            scratch_shapes=[pltpu.VMEM((8, d_model, f_loc), F32), dma((8,))],
            compiler_params=pltpu.CompilerParams(vmem_limit_bytes=56 * 2**20),
        )(h, da, xr, dyr, out, dx, dwg)
        return out, dx, dwi, dwo, dwg

    in_specs = (row_spec, row_spec, P(None, None), P("ep", None, "tp"), P("ep", "tp", None), P(("dp", "ep")))
    out_specs = (row_spec, row_spec, P(("dp", "ep"), None, "tp"), P(("dp", "ep"), "tp", None), P("dp", None))
    return jax.shard_map(local_block, mesh=mesh, in_specs=in_specs, out_specs=out_specs, check_vma=False)
```

time: 151 us -> 85.9 us (0.57)
  blocking collectives: 86.1 us -> 0 us
  Pallas kernels: 0 us -> 81.7 us
  matrix products: 21.8 us -> 0 us
  starting transfers between devices: 14.9 us -> 0 us
  waiting for transfers between devices: 10.5 us -> 0 us
  local copies, waits for them, and re-layouts: 10.9 us -> 3.31 us
  other arithmetic: 5.82 us -> 0 us
    psum x2 -> x0, blocking collectives: 86.1 us -> none  [the longest x1 73.6 us: local_block(): y_rows = lax.psum(y_part, 'tp').astype(jnp.bfloat16)]
    pallas_call x0 -> x2, Pallas kernels: none -> 81.7 us  [the longest x1 71.7 us: local_block(): pl.pallas_call(functools.partial(moe_kernel, cap), out_shape=out_shape, i...]
    dot_general x9 -> x0, matrix products: 21.8 us -> none  [the longest x1 5.2 us: local_block(): jnp.einsum('erf,erd->efd', hidden, dy_rows, preferred_element_type=jnp.fl...]
    all_to_all x4 -> x0, starting transfers between devices: 14.9 us -> none  [the longest x2 7.77 us: dispatch(): recv_buf = lax.all_to_all(send_buf, 'ep', 0, 2, tiled=True)]
    all_to_all x4 -> x0, waiting for transfers between devices: 10.5 us -> none  [the longest x2 8.47 us: dispatch(): recv_buf = lax.all_to_all(send_buf, 'ep', 0, 2, tiled=True)]
    convert_element_type x2 -> x0, local copies, waits for them, and re-layouts: 3.1 us -> none  [the longest x1 2.05 us: local_block(): y_rows = lax.psum(y_part, 'tp').astype(jnp.bfloat16)]
    gather x2 -> x0, local copies, waits for them, and re-layouts: 2.37 us -> none  [combine(): return jnp.take(padded, slot_index, axis=0)]
    reshape x6 -> x0, local copies, waits for them, and re-layouts: 2.34 us -> none  [the longest x4 2.14 us: dispatch(): slot_buf[:n_slots].reshape(ep_size, local_experts, capacity, d_model)]
  transfers between devices with their start and end apart: 4 -> 0, of which waited for: 3 -> 0; matrix products, arithmetic and copies ran while one was open for 11% -> 0% of each run, Pallas kernels for 0% -> 0%
where the time goes in v1:
time: 85.9 us; the launch traced here: 85.6 us
  Pallas kernels  81.7 us (95%)
  local copies, waits for them, and re-layouts  3.31 us (4%)
    pallas_call x1, Pallas kernels, local_block(): pl.pallas_call(functools.partial(moe_kernel, cap), out_shape=out_shape, i...  71.7 us
    pallas_call x1, Pallas kernels, local_block(): pl.pallas_call(functools.partial(grads_kernel, cap), out_shape=(S((n_tok,...  9.97 us
    pallas_call x1, local copies, waits for them, and re-layouts, local_block(): pl.pallas_call(functools.partial(grads_kernel, cap), out_shape=(S((n_tok,...  1.75 us

profile of v1, /device:TPU:0, one launch (start us, length us, event | category | flops | bytes accessed | tf_op | source)
XLA Modules:
  0.0 85.6 jit_solution(9108582146905458916)
XLA Ops:
  0.6 1.6 %copy.11.wg_ref = bf16[768,16]{1,0:T(8,128)(2,1)} copy(bf16[768,16]{0,1:T(8,128)(2,1)} %param.8) | data formatting | bytes 49152 | tf_op args[2]
  2.2 71.7 %shard_map.101 = (bf16[256,768]{1,0:T(8,128)(2,1)}, bf16[256,768]{1,0:T(8,128)(2,1)}, f32[16,768]{1,0:T(8,128)}, bf16[2,160,768]{2,1,0:T(8,128)(2,1)}, bf16[2,16...) custom-call(s32[1,256]{1,0:T(1,128)} %bitcast.1, ...), custom_call_target="tpu_custom_call" | custom-call | tf_op jit(solution)/shard_map/pallas_call | solution.py:375
  73.9 10.0 %shard_map.102 = (bf16[256,768]{1,0:T(8,128)(2,1)}, bf16[256,768]{1,0:T(8,128)(2,1)}, f32[4,768,768]{2,1,0:T(8,128)}, f32[4,768,768]{2,1,0:T(8,128)}, f32[768,16]{1,0:T(8,128)}) custom-call(bf16[2,160,768]{2,1,0:T(8,128)(2,1)} %get-tuple-element.12.h_ref, bf16[2,160,768]{2,1,0:T(8,128)(2,1)} %get-tuple-element.13.da_ref, ...), custom_call_target="tpu_custom_call" | custom-call | tf_op jit(solution)/shard_map/pallas_call | solution.py:383
  83.9 1.8 %copy.12 = f32[768,16]{0,1:T(8,128)} copy(f32[768,16]{1,0:T(8,128)} %get-tuple-element.23) | data formatting | bytes 98304 | tf_op jit(solution)/shard_map/pallas_call | solution.py:383

commit v2 on v0

v2 whole, which is shorter than its diff:
```python
import functools

import jax
import jax.numpy as jnp
from jax import lax
from jax.experimental import pallas as pl
from jax.experimental.pallas import tpu as pltpu
from jax.sharding import PartitionSpec as P

MESH = pl.DeviceIdType.MESH
F32, BF16 = jnp.float32, jnp.bfloat16
GELU_C = 0.7978845608028654
GELU_K = 0.044715
N_EP, N_TP, N_PAIR, N_BACK = 4, 4, 2, 4


def dot(a, b, dims=((1,), (0,))):
    return lax.dot_general(a, b, (dims, ((), ())), preferred_element_type=F32)


def pair_masks(rows, block, cap):
    row = lax.broadcasted_iota(jnp.int32, (rows, 1), 0)
    first = lax.rem(row, block) < cap
    return jnp.where(first, 1.0, 0.0).astype(BF16), jnp.where(first, 0.0, 1.0).astype(BF16)


def moe_kernel(
    cap,
    ids_hbm, wg_hbm, x_hbm, gy_hbm, wi_hbm, wo_hbm,
    out_v, dx_v, dwg_v, dwi_v, dwo_v,
    ids_ref, wg_ref, x_v, gy_v, wi_v, wo_v,
    onehot_slots, router_v, send_v, recv_v, act_v, h_v, da_v,
    part_v, rs_in, red_v, slots_v,
    dwg_part, dwg_in,
    load_sem, sent_sem, disp_recv, rs_recv, hop_recv, ag_recv, wg_recv,
):
    block = 2 * cap
    rows = N_EP * block
    n_tok, d_model = x_v.shape
    n_exp = wg_ref.shape[0]
    half = d_model // 2
    z, j = lax.axis_index("tp"), lax.axis_index("ep")
    right, left = lax.rem(z + 1, N_TP), lax.rem(z + N_TP - 1, N_TP)
    ep_peer = [lax.rem(j + k, N_EP) for k in range(N_EP)]

    def remote(kind, src, dst, rsem, **dev):
        return pltpu.make_async_remote_copy(
            src_ref=src, dst_ref=dst, send_sem=sent_sem.at[kind], recv_sem=rsem, device_id=dev, device_id_type=MESH
        )

    def wait_bytes(ref, sem):
        pltpu.make_async_copy(ref, ref, sem).wait()

    load_x = pltpu.make_async_copy(x_hbm, x_v, load_sem.at[0])
    load_gy = pltpu.make_async_copy(gy_hbm, gy_v, load_sem.at[1])
    load_wi = [pltpu.make_async_copy(wi_hbm.at[pl.ds(2 * p, 2)], wi_v.at[pl.ds(2 * p, 2)], load_sem.at[2 + p]) for p in range(2)]
    load_wo = [pltpu.make_async_copy(wo_hbm.at[pl.ds(2 * p, 2)], wo_v.at[pl.ds(2 * p, 2)], load_sem.at[4 + p]) for p in range(2)]
    load_ids = pltpu.make_async_copy(ids_hbm, ids_ref, load_sem.at[6])
    load_wg = pltpu.make_async_copy(wg_hbm, wg_ref, load_sem.at[7])
    for load in (load_ids, load_x, load_wg, load_gy):
        load.start()

    barrier = pltpu.get_barrier_semaphore()
    for dev in [{"tp": right}, {"tp": left}] + [{"ep": ep_peer[k]} for k in range(1, N_EP)]:
        pl.semaphore_signal(barrier, inc=1, device_id=dev, device_id_type=MESH)

    for p in range(2):
        load_wi[p].start()
        load_wo[p].start()

    load_ids.wait()
    ids = ids_ref[...]
    chosen = ids == lax.broadcasted_iota(jnp.int32, (n_exp, n_tok), 0)
    onehot = jnp.where(chosen, 1.0, 0.0)
    before = lax.broadcasted_iota(jnp.int32, (n_tok, n_tok), 0) < lax.broadcasted_iota(jnp.int32, (n_tok, n_tok), 1)
    counts = dot(onehot.astype(BF16), jnp.where(before, 1.0, 0.0).astype(BF16))
    pos = jnp.sum(counts * onehot, axis=0, keepdims=True)
    base = ((ids >> 1) & 1) * rows + (ids >> 2) * block + (ids & 1) * cap
    slot = jnp.where(pos < cap, base.astype(F32) + pos, -1.0)
    slot_iota = lax.broadcasted_iota(jnp.int32, (2 * rows, n_tok), 0).astype(F32)
    onehot_slots[...] = jnp.where(slot_iota == slot, 1.0, 0.0).astype(BF16)

    def dispatch(t, tok_rows):
        packed = dot(onehot_slots[...], tok_rows).astype(BF16)
        send_v[t] = packed.reshape(2, N_EP, block, d_model)

    def disp_copy(t, p, k):
        return remote(
            0, send_v.at[t, p, ep_peer[k]], recv_v.at[t, p, j], disp_recv.at[t, p], ep=ep_peer[k]
        )

    def start_dispatch(t):
        for p in range(N_PAIR):
            for k in (2, 1, 3):
                disp_copy(t, p, k).start()
        for p in range(N_PAIR):
            recv_v[t, p, j] = send_v[t, p, j]

    def route_x():
        load_x.wait()
        dispatch(0, x_v[...])

    def route_dy():
        load_wg.wait()
        logits = dot(wg_ref[...], x_v[...], ((1,), (1,)))
        expd = jnp.exp(logits - jnp.max(logits, axis=0, keepdims=True))
        prob = expd / jnp.sum(expd, axis=0, keepdims=True)
        gate_row = jnp.sum(jnp.where(chosen, prob, 0.0), axis=0, keepdims=True)
        router_v[...] = prob * (onehot - gate_row)
        gate = jnp.transpose(jnp.broadcast_to(gate_row, (128, n_tok)))[:, :1]
        load_gy.wait()
        dispatch(1, (gate * gy_v[...].astype(F32)).astype(BF16))
        return gate

    def meet():
        pl.semaphore_wait(barrier, 5)

    def step(name, f, *a):
        with jax.named_scope(name + "".join(map(str, a))):
            return f(*a)

    step("route_x", route_x)
    step("meet", meet)
    start_dispatch(0)
    gate_v = step("route_dy", route_dy)
    start_dispatch(1)

    mask0, mask1 = pair_masks(rows, block, cap)

    def wait_rows(t, p):
        wait_bytes(recv_v.at[t, p, pl.ds(0, N_EP - 1)], disp_recv.at[t, p])
        return recv_v[t, p].reshape(rows, d_model)

    def pair_dot(lhs, w_ref, p, dims=((1,), (0,))):
        return dot(lhs * mask0, w_ref[2 * p], dims) + dot(lhs * mask1, w_ref[2 * p + 1], dims)

    place = [z, N_TP - 1 - z]
    ahead, behind = [right, left], [left, right]

    def rs_copy(i, h, q):
        return remote(1, part_v.at[i, h, q], rs_in.at[i, h, q], rs_recv.at[i, h, q], tp=ahead[h])

    def rs_start(i, part):
        part_v[i, 0] = part[:, :half].reshape(N_EP, block, half)
        part_v[i, 1] = part[:, half:].reshape(N_EP, block, half)
        for h in (0, 1):
            @pl.when(place[h] == 0)
            def _():
                for q in range(N_EP):
                    rs_copy(i, h, q).start()

    def rs_relay(at, i, q):
        for h in (0, 1):
            @pl.when(place[h] == at)
            def _():
                rs_copy(i, h, q).wait_recv()
                part_v[i, h, q] = part_v[i, h, q] + rs_in[i, h, q]
                rs_copy(i, h, q).start()

    def hop_copy(i, h, q):
        return remote(2, red_v.at[i, q], slots_v.at[i, h, j], hop_recv.at[i], ep=q)

    def rs_final(i, q):
        for h in (0, 1):
            @pl.when(place[h] == N_TP - 1)
            def _():
                rs_copy(i, h, q).wait_recv()
                red_v[i, q] = (part_v[i, h, q] + rs_in[i, h, q]).astype(BF16)

                @pl.when(j != q)
                def _():
                    hop_copy(i, h, q).start()

                @pl.when(j == q)
                def _():
                    slots_v[i, h, j] = red_v[i, q]

    def ag_copy(i, h, n):
        part = slots_v.at[i, h, pl.ds(n * (N_EP // N_BACK), N_EP // N_BACK)]
        return remote(3, part, part, ag_recv.at[i, h, n], tp=behind[h])

    def ag_root(i, q):
        for h in (0, 1):
            @pl.when((place[h] == N_TP - 1) & (j == q))
            def _():
                wait_bytes(slots_v.at[i, h, pl.ds(0, N_EP - 1)], hop_recv.at[i])
                for n in range(N_BACK):
                    ag_copy(i, h, n).start()

    def ag_forward(at, i, n):
        for h in (0, 1):
            @pl.when(place[h] == at)
            def _():
                ag_copy(i, h, n).wait_recv()
                ag_copy(i, h, n).start()

    def ag_last(i):
        for h in (0, 1):
            @pl.when(place[h] == 0)
            def _():
                for n in range(N_BACK):
                    ag_copy(i, h, n).wait_recv()

    def forward(p):
        load_wi[p].wait()
        xr = wait_rows(0, p)
        a = pair_dot(xr, wi_v, p)
        act_v[p] = a
        h = (0.5 * a * (1.0 + jnp.tanh(GELU_C * (a + GELU_K * a * a * a)))).astype(BF16)
        h_v[p] = h
        load_wo[p].wait()
        rs_start(p, pair_dot(h, wo_v, p))

    def backward_act(p):
        dyr = wait_rows(1, p)
        dh = pair_dot(dyr, wo_v, p, ((1,), (1,)))
        a = act_v[p]
        a2 = a * a
        th = jnp.tanh(GELU_C * (a + GELU_K * a2 * a))
        slope = 0.5 * (1.0 + th) + 0.5 * a * (1.0 - th * th) * (GELU_C * (1.0 + 3.0 * GELU_K * a2))
        da_v[p] = (dh * slope).astype(BF16)

    def backward_in(p):
        rs_start(2 + p, pair_dot(da_v[p], wi_v, p, ((1,), (1,))))

    def combine(t):
        halves = [
            jnp.concatenate([slots_v[2 * t + p, h].reshape(rows, half) for p in range(N_PAIR)], axis=0) for h in (0, 1)
        ]
        return dot(onehot_slots[...], jnp.concatenate(halves, axis=1), ((0,), (0,)))

    def weight_grad(n):
        e = n // 2
        p, mask = e // 2, (mask0, mask1)[e % 2]
        if n % 2 == 0:
            dwo_v[e] = dot(h_v[p] * mask, recv_v[1, p].reshape(rows, d_model), ((0,), (0,)))
        else:
            dwi_v[e] = dot(recv_v[0, p].reshape(rows, d_model) * mask, da_v[p], ((0,), (0,)))

    def first(k):
        step("relay1_", rs_relay, 1, k // 4, k % 4)

    def second(k):
        step("relay2_", rs_relay, 2, k // 4, k % 4)

    def last(k):
        step("final_", rs_final, k // 4, k % 4)

    step("forward", forward, 0)
    step("forward", forward, 1)
    first(0)
    step("bwd_act", backward_act, 0)
    first(1)
    step("bwd_in", backward_in, 0)
    first(2)
    second(0)
    step("bwd_act", backward_act, 1)
    first(3)
    second(1)
    step("bwd_in", backward_in, 1)

    def back(at, i, pieces=range(N_BACK)):
        for n in pieces:
            step(f"ag_fwd{at}_", ag_forward, at, i, n)

    for k in range(4, 16):
        first(k)
        second(k - 2)
        if 6 <= k < 14:
            step("weight_grad", weight_grad, k - 6)
    back(2, 0, [0, 1])
    second(14)
    back(2, 0, [2, 3])
    second(15)
    for k in range(16):
        last(k)
        if k >= 2:
            step("ag_root", ag_root, (k - 2) // 4, (k - 2) % 4)
    step("ag_root", ag_root, 3, 2)
    step("ag_root", ag_root, 3, 3)
    for n in range(N_BACK):
        back(2, 1, [n])
        back(1, 0, [n])
    for n in range(N_BACK):
        back(2, 2, [n])
        back(1, 1, [n])
    step("ag_last", ag_last, 0)
    step("ag_last", ag_last, 1)

    def wg_copy(k):
        return remote(4, dwg_part, dwg_in.at[k - 1], wg_recv, ep=ep_peer[k])

    def finish_y():
        y_tok = combine(0)
        out_v[...] = (gate_v * y_tok).astype(BF16)
        d_gate = jnp.sum(gy_v[...].astype(F32) * y_tok, axis=1, keepdims=True)
        d_gate_row = jnp.transpose(jnp.broadcast_to(d_gate, (n_tok, 128)))[:1]
        d_logits = d_gate_row * router_v[...]
        dwg_part[...] = dot(d_logits.astype(BF16), x_v[...])
        for k in range(1, N_EP):
            wg_copy(k).start()
        return dot(jnp.transpose(d_logits).astype(BF16), wg_ref[...])

    def finish_wg():
        wait_bytes(dwg_in, wg_recv)
        dwg_v[...] = (dwg_part[...] + dwg_in[1]) + (dwg_in[0] + dwg_in[2])

    def finish_s():
        dx_v[...] = (combine(1) + router_grad).astype(BF16)

    router_grad = step("finish_y", finish_y)
    for n in range(N_BACK):
        back(2, 3, [n])
        back(1, 2, [n])
    step("finish_wg", finish_wg)
    back(1, 3)
    step("ag_last", ag_last, 2)
    step("ag_last", ag_last, 3)
    step("finish_s", finish_s)

    def drain():
        wait_bytes(part_v.at[pl.ds(0, N_EP - 1), 0], sent_sem.at[0])
        wait_bytes(dwg_in, sent_sem.at[4])

        @pl.when((z == 0) | (z == N_TP - 1))
        def _():
            wait_bytes(part_v.at[:, 0], sent_sem.at[1])
            wait_bytes(red_v.at[:, pl.ds(0, N_EP - 1)], sent_sem.at[2])
            wait_bytes(slots_v.at[:, 0], sent_sem.at[3])

        @pl.when((z != 0) & (z != N_TP - 1))
        def _():
            wait_bytes(part_v, sent_sem.at[1])
            wait_bytes(slots_v, sent_sem.at[3])

    step("drain", drain)


def store_kernel(out_v, dx_v, dwg_v, dwi_v, dwo_v, out_hbm, dx_hbm, dwg_hbm, dwi_hbm, dwo_hbm, sem):
    pairs = [(dwi_v.at[e], dwi_hbm.at[e]) for e in range(4)] + [(dwo_v.at[e], dwo_hbm.at[e]) for e in range(4)]
    pairs += [(out_v, out_hbm), (dx_v, dx_hbm), (dwg_v, dwg_hbm)]
    copies = [pltpu.make_async_copy(src, dst, sem.at[n]) for n, (src, dst) in enumerate(pairs)]
    for cp in copies:
        cp.start()
    for cp in copies:
        cp.wait()


def solution(mesh):
    row_spec = P(("dp", "ep"), None)

    def local_block(tokens, grad_out, w_router, w_in, w_out, expert_ids):
        n_tok, d_model = tokens.shape
        n_exp = w_router.shape[1]
        n_loc, _, f_loc = w_in.shape
        cap = (6 * n_tok + 5 * n_exp - 1) // (5 * n_exp)
        block, rows, half = 2 * cap, 8 * cap, d_model // 2
        S = jax.ShapeDtypeStruct
        any_spec, vmem_spec = pl.BlockSpec(memory_space=pl.ANY), pl.BlockSpec(memory_space=pltpu.VMEM)
        dma = pltpu.SemaphoreType.DMA
        out_shape = (
            S((n_tok, d_model), BF16), S((n_tok, d_model), BF16), S((n_exp, d_model), F32),
            S((n_loc, d_model, f_loc), F32), S((n_loc, f_loc, d_model), F32),
        )
        held = tuple(pltpu.VMEM(s.shape, s.dtype) for s in out_shape)
        scratch = [
            pltpu.VMEM((1, n_tok), jnp.int32), pltpu.VMEM((n_exp, d_model), BF16),
            pltpu.VMEM((n_tok, d_model), BF16), pltpu.VMEM((n_tok, d_model), BF16),
            pltpu.VMEM(w_in.shape, BF16), pltpu.VMEM(w_out.shape, BF16),
            pltpu.VMEM((2 * rows, n_tok), BF16), pltpu.VMEM((n_exp, n_tok), F32),
            pltpu.VMEM((2, 2, N_EP, block, d_model), BF16), pltpu.VMEM((2, 2, N_EP, block, d_model), BF16),
            pltpu.VMEM((2, rows, f_loc), F32), pltpu.VMEM((2, rows, f_loc), BF16), pltpu.VMEM((2, rows, f_loc), BF16),
            pltpu.VMEM((4, 2, N_EP, block, half), F32), pltpu.VMEM((4, 2, N_EP, block, half), F32),
            pltpu.VMEM((4, N_EP, block, half), BF16), pltpu.VMEM((4, 2, N_EP, block, half), BF16),
            pltpu.VMEM((n_exp, d_model), F32), pltpu.VMEM((3, n_exp, d_model), F32),
            dma((8,)), dma((5,)), dma((2, 2)), dma((4, 2, N_EP)), dma((4,)), dma((4, 2, N_BACK)), dma,
        ]
        results = pl.pallas_call(
            functools.partial(moe_kernel, cap),
            out_shape=held,
            in_specs=[any_spec] * 6,
            out_specs=(vmem_spec,) * 5,
            scratch_shapes=scratch,
            compiler_params=pltpu.CompilerParams(collective_id=0, has_side_effects=True, vmem_limit_bytes=24 * 2**20),
        )(*[
            pltpu.with_memory_space_constraint(r, pltpu.HBM)
            for r in (expert_ids.reshape(1, n_tok), w_router.T, tokens, grad_out, w_in, w_out)
        ])
        out, dx, dwg, dwi, dwo = pl.pallas_call(
            store_kernel,
            out_shape=out_shape,
            in_specs=[any_spec] * 5,
            out_specs=(any_spec,) * 5,
            scratch_shapes=[dma((11,))],
            compiler_params=pltpu.CompilerParams(vmem_limit_bytes=2**20),
        )(*[pltpu.with_memory_space_constraint(r, pltpu.VMEM) for r in results])
        return out, dx, dwi, dwo, dwg.T

    in_specs = (row_spec, row_spec, P(None, None), P("ep", None, "tp"), P("ep", "tp", None), P(("dp", "ep")))
    out_specs = (row_spec, row_spec, P(("dp", "ep"), None, "tp"), P(("dp", "ep"), "tp", None), P("dp", None))
    return jax.shard_map(local_block, mesh=mesh, in_specs=in_specs, out_specs=out_specs, check_vma=False)
```

time: 151 us -> 62.1 us (0.41)
  blocking collectives: 86.1 us -> 0 us
  Pallas kernels: 0 us -> 61.3 us
  matrix products: 21.8 us -> 0 us
  starting transfers between devices: 14.9 us -> 0 us
  local copies, waits for them, and re-layouts: 10.9 us -> 0 us
  waiting for transfers between devices: 10.5 us -> 0 us
  other arithmetic: 5.82 us -> 0 us
    psum x2 -> x0, blocking collectives: 86.1 us -> none  [the longest x1 73.6 us: local_block(): y_rows = lax.psum(y_part, 'tp').astype(jnp.bfloat16)]
    pallas_call x0 -> x2, Pallas kernels: none -> 61.3 us  [the longest x1 54.6 us: local_block(): pl.pallas_call(functools.partial(moe_kernel, cap), out_shape=held, in_spe...]
    dot_general x9 -> x0, matrix products: 21.8 us -> none  [the longest x1 5.2 us: local_block(): jnp.einsum('erf,erd->efd', hidden, dy_rows, preferred_element_type=jnp.fl...]
    all_to_all x4 -> x0, starting transfers between devices: 14.9 us -> none  [the longest x2 7.77 us: dispatch(): recv_buf = lax.all_to_all(send_buf, 'ep', 0, 2, tiled=True)]
    all_to_all x4 -> x0, waiting for transfers between devices: 10.5 us -> none  [the longest x2 8.47 us: dispatch(): recv_buf = lax.all_to_all(send_buf, 'ep', 0, 2, tiled=True)]
    convert_element_type x2 -> x0, local copies, waits for them, and re-layouts: 3.1 us -> none  [the longest x1 2.05 us: local_block(): y_rows = lax.psum(y_part, 'tp').astype(jnp.bfloat16)]
    gather x2 -> x0, local copies, waits for them, and re-layouts: 2.37 us -> none  [combine(): return jnp.take(padded, slot_index, axis=0)]
    reshape x6 -> x0, local copies, waits for them, and re-layouts: 2.34 us -> none  [the longest x4 2.14 us: dispatch(): slot_buf[:n_slots].reshape(ep_size, local_experts, capacity, d_model)]
  transfers between devices with their start and end apart: 4 -> 0, of which waited for: 3 -> 0; matrix products, arithmetic and copies ran while one was open for 11% -> 0% of each run, Pallas kernels for 0% -> 0%
where the time goes in v2:
time: 62.1 us; the launch traced here: 62 us
  Pallas kernels  61.3 us (99%)
  between operations  0.64 us (1%)
    pallas_call x1, Pallas kernels, local_block(): pl.pallas_call(functools.partial(moe_kernel, cap), out_shape=held, in_spe...  54.6 us
    pallas_call x1, Pallas kernels, local_block(): pl.pallas_call(store_kernel, out_shape=out_shape, in_specs=[any_spec] * 5...  6.78 us

profile of v2, /device:TPU:0, one launch (start us, length us, event | category | flops | bytes accessed | tf_op | source)
XLA Modules:
  0.0 62.0 jit_solution(4969378134332087302)
XLA Ops:
  0.6 54.6 %shard_map.101 = (bf16[256,768]{1,0:T(8,128)(2,1)S(1)}, bf16[256,768]{1,0:T(8,128)(2,1)S(1)}, f32[16,768]{1,0:T(8,128)S(1)}, f32[4,768,768]{2,1,0:T(8,128)S(1)}, f32[4,768,768]{2,1,0:T(8,128)S(1)}) custom-call(s32[1,256]{1,0:T(1,128)} %bitcast.4, bf16[16,768]{1,0:T(8,128)(2,1)} %bitcast.3, bf16[256,768]{1,0:T(8,128)(2,1)} %x_hbm.1, bf16[256,768]{1,0:T(8,128)(2,1)} %gy_hbm.1, ...), custom_call_target="tpu_custom_call" | custom-call | tf_op jit(solution)/shard_map/pallas_call | solution.py:378
  55.2 6.8 %shard_map.102 = (bf16[256,768]{1,0:T(8,128)(2,1)}, bf16[256,768]{1,0:T(8,128)(2,1)}, f32[16,768]{1,0:T(8,128)}, f32[4,768,768]{2,1,0:T(8,128)}, f32[4,768,768]{2,1,0:T(8,128)}) custom-call(bf16[256,768]{1,0:T(8,128)(2,1)S(1)} %get-tuple-element.15.out_v, bf16[256,768]{1,0:T(8,128)(2,1)S(1)} %get-tuple-element.16.dx_v, ...), custom_call_target="tpu_custom_call" | custom-call | tf_op jit(solution)/shard_map/pallas_call | solution.py:389

commit v3 on v2

--- a/solution.py
+++ b/solution.py
@@ -11,7 +11,7 @@
 F32, BF16 = jnp.float32, jnp.bfloat16
 GELU_C = 0.7978845608028654
 GELU_K = 0.044715
-N_EP, N_TP, N_PAIR, N_BACK = 4, 4, 2, 4
+N_EP, N_TP, N_PAIR = 4, 4, 2
 
 
 def dot(a, b, dims=((1,), (0,))):
@@ -32,7 +32,7 @@
     onehot_slots, router_v, send_v, recv_v, act_v, h_v, da_v,
     part_v, rs_in, red_v, slots_v,
     dwg_part, dwg_in,
-    load_sem, sent_sem, disp_recv, rs_recv, hop_recv, ag_recv, wg_recv,
+    load_sem, sent_sem, disp_recv, rs_recv, hop_recv, turn_recv, back_recv, wg_recv,
 ):
     block = 2 * cap
     rows = N_EP * block
@@ -41,7 +41,10 @@
     half = d_model // 2
     z, j = lax.axis_index("tp"), lax.axis_index("ep")
     right, left = lax.rem(z + 1, N_TP), lax.rem(z + N_TP - 1, N_TP)
-    ep_peer = [lax.rem(j + k, N_EP) for k in range(N_EP)]
+    chip = j // 2
+    near = j + 1 - 2 * lax.rem(j, 2)
+    ep_peer = [near, lax.rem(j + 2, N_EP), lax.rem(near + 2, N_EP)]
+    side = [2 * chip, 2 - 2 * chip]
 
     def remote(kind, src, dst, rsem, **dev):
         return pltpu.make_async_remote_copy(
@@ -61,8 +64,20 @@
         load.start()
 
     barrier = pltpu.get_barrier_semaphore()
-    for dev in [{"tp": right}, {"tp": left}] + [{"ep": ep_peer[k]} for k in range(1, N_EP)]:
+    pair_z = z + 1 - 2 * lax.rem(z, 2)
+    at_end = (z == 0) | (z == N_TP - 1)
+
+    def greet(**dev):
         pl.semaphore_signal(barrier, inc=1, device_id=dev, device_id_type=MESH)
+
+    for peer in ep_peer:
+        greet(ep=peer)
+    for peer in [j] + ep_peer:
+        greet(tp=pair_z, ep=peer)
+
+    @pl.when(jnp.logical_not(at_end))
+    def _():
+        greet(tp=N_TP - 1 - z)
 
     for p in range(2):
         load_wi[p].start()
@@ -85,13 +100,14 @@
         send_v[t] = packed.reshape(2, N_EP, block, d_model)
 
     def disp_copy(t, p, k):
-        return remote(
-            0, send_v.at[t, p, ep_peer[k]], recv_v.at[t, p, j], disp_recv.at[t, p], ep=ep_peer[k]
-        )
+        peer = ep_peer[k]
+        return remote(0, send_v.at[t, p, peer], recv_v.at[t, p, j], disp_recv.at[t, p, min(k, 1)], ep=peer)
 
     def start_dispatch(t):
         for p in range(N_PAIR):
-            for k in (2, 1, 3):
+            disp_copy(t, p, 0).start()
+        for p in range(N_PAIR):
+            for k in (1, 2):
                 disp_copy(t, p, k).start()
         for p in range(N_PAIR):
             recv_v[t, p, j] = send_v[t, p, j]
@@ -113,7 +129,13 @@
         return gate
 
     def meet():
-        pl.semaphore_wait(barrier, 5)
+        @pl.when(at_end)
+        def _():
+            pl.semaphore_wait(barrier, 7)
+
+        @pl.when(jnp.logical_not(at_end))
+        def _():
+            pl.semaphore_wait(barrier, 8)
 
     def step(name, f, *a):
         with jax.named_scope(name + "".join(map(str, a))):
@@ -126,13 +148,21 @@
     start_dispatch(1)
 
     mask0, mask1 = pair_masks(rows, block, cap)
-
-    def wait_rows(t, p):
-        wait_bytes(recv_v.at[t, p, pl.ds(0, N_EP - 1)], disp_recv.at[t, p])
-        return recv_v[t, p].reshape(rows, d_model)
+    part_rows = 2 * block
+
+    def rows_from(t, p, far):
+        return recv_v[t, p, pl.ds(side[far], 2)].reshape(part_rows, d_model)
+
+    def wait_rows(t, p, far):
+        wait_bytes(recv_v.at[t, p, pl.ds(0, 1 + far)], disp_recv.at[t, p, far])
+        return rows_from(t, p, far)
+
+    def all_rows(t, p):
+        return jnp.concatenate([rows_from(t, p, far) for far in (0, 1)], axis=0)
 
     def pair_dot(lhs, w_ref, p, dims=((1,), (0,))):
-        return dot(lhs * mask0, w_ref[2 * p], dims) + dot(lhs * mask1, w_ref[2 * p + 1], dims)
+        first, second = lhs * mask0[: lhs.shape[0]], lhs * mask1[: lhs.shape[0]]
+        return dot(first, w_ref[2 * p], dims) + dot(second, w_ref[2 * p + 1], dims)
 
     place = [z, N_TP - 1 - z]
     ahead, behind = [right, left], [left, right]
@@ -140,16 +170,18 @@
     def rs_copy(i, h, q):
         return remote(1, part_v.at[i, h, q], rs_in.at[i, h, q], rs_recv.at[i, h, q], tp=ahead[h])
 
-    def rs_start(i, part):
-        part_v[i, 0] = part[:, :half].reshape(N_EP, block, half)
-        part_v[i, 1] = part[:, half:].reshape(N_EP, block, half)
+    def rs_start(i, far, part):
+        where = pl.ds(side[far], 2)
+        part_v[i, 0, where] = part[:, :half].reshape(2, block, half)
+        part_v[i, 1, where] = part[:, half:].reshape(2, block, half)
         for h in (0, 1):
             @pl.when(place[h] == 0)
             def _():
-                for q in range(N_EP):
-                    rs_copy(i, h, q).start()
-
-    def rs_relay(at, i, q):
+                for b in range(2):
+                    rs_copy(i, h, side[far] + b).start()
+
+    def rs_relay(at, i, far, b):
+        q = side[far] + b
         for h in (0, 1):
             @pl.when(place[h] == at)
             def _():
@@ -157,178 +189,209 @@
                 part_v[i, h, q] = part_v[i, h, q] + rs_in[i, h, q]
                 rs_copy(i, h, q).start()
 
-    def hop_copy(i, h, q):
-        return remote(2, red_v.at[i, q], slots_v.at[i, h, j], hop_recv.at[i], ep=q)
-
-    def rs_final(i, q):
+    def hop_copy(i, h, q, far):
+        return remote(2, red_v.at[i, q], slots_v.at[i, h, j], hop_recv.at[i, far], ep=q)
+
+    def turn_copy(i, h, q, far):
+        return remote(5, red_v.at[i, q], slots_v.at[i, h, j], turn_recv.at[i, far], tp=behind[h], ep=q)
+
+    def rs_final(i, far, b):
+        q = side[far] + b
         for h in (0, 1):
             @pl.when(place[h] == N_TP - 1)
             def _():
                 rs_copy(i, h, q).wait_recv()
                 red_v[i, q] = (part_v[i, h, q] + rs_in[i, h, q]).astype(BF16)
-
-                @pl.when(j != q)
-                def _():
-                    hop_copy(i, h, q).start()
-
-                @pl.when(j == q)
-                def _():
-                    slots_v[i, h, j] = red_v[i, q]
-
-    def ag_copy(i, h, n):
-        part = slots_v.at[i, h, pl.ds(n * (N_EP // N_BACK), N_EP // N_BACK)]
-        return remote(3, part, part, ag_recv.at[i, h, n], tp=behind[h])
-
-    def ag_root(i, q):
-        for h in (0, 1):
-            @pl.when((place[h] == N_TP - 1) & (j == q))
-            def _():
-                wait_bytes(slots_v.at[i, h, pl.ds(0, N_EP - 1)], hop_recv.at[i])
-                for n in range(N_BACK):
-                    ag_copy(i, h, n).start()
-
-    def ag_forward(at, i, n):
-        for h in (0, 1):
-            @pl.when(place[h] == at)
-            def _():
-                ag_copy(i, h, n).wait_recv()
-                ag_copy(i, h, n).start()
-
-    def ag_last(i):
+                turn_copy(i, h, q, far).start()
+                if far:
+                    hop_copy(i, h, q, far).start()
+                else:
+                    @pl.when(j != q)
+                    def _():
+                        hop_copy(i, h, q, far).start()
+
+                    @pl.when(j == q)
+                    def _():
+                        slots_v[i, h, j] = red_v[i, q]
+
+    def hop_wait(i):
+        for h in (0, 1):
+            @pl.when(place[h] == N_TP - 1)
+            def _():
+                for far in (0, 1):
+                    wait_bytes(slots_v.at[i, h, pl.ds(0, 1 + far)], hop_recv.at[i, far])
+
+    def back_copy(i, h, far):
+        part = slots_v.at[i, h, pl.ds(side[far], 2)]
+        return remote(3, part, part, back_recv.at[i, far], tp=behind[h])
+
+    def back_first(i, far):
+        for h in (0, 1):
+            @pl.when(place[h] == 2)
+            def _():
+                wait_bytes(slots_v.at[i, h, pl.ds(0, 2)], turn_recv.at[i, far])
+                back_copy(i, h, far).start()
+
+    def back_second(i, far):
+        for h in (0, 1):
+            @pl.when(place[h] == 1)
+            def _():
+                back_copy(i, h, far).wait_recv()
+                back_copy(i, h, far).start()
+
+    def back_last(i, far):
         for h in (0, 1):
             @pl.when(place[h] == 0)
             def _():
-                for n in range(N_BACK):
-                    ag_copy(i, h, n).wait_recv()
-
-    def forward(p):
-        load_wi[p].wait()
-        xr = wait_rows(0, p)
-        a = pair_dot(xr, wi_v, p)
-        act_v[p] = a
+                back_copy(i, h, far).wait_recv()
+
+    def by_token(t):
+        halves = [
+            jnp.concatenate([slots_v[2 * t + p, h].reshape(rows, half) for p in range(N_PAIR)], axis=0) for h in (0, 1)
+        ]
+        return dot(onehot_slots[...], jnp.concatenate(halves, axis=1), ((0,), (0,)))
+
+    def forward(p, far):
+        if far == 0:
+            load_wi[p].wait()
+        a = pair_dot(wait_rows(0, p, far), wi_v, p)
+        act_v[p, far] = a
         h = (0.5 * a * (1.0 + jnp.tanh(GELU_C * (a + GELU_K * a * a * a)))).astype(BF16)
-        h_v[p] = h
-        load_wo[p].wait()
-        rs_start(p, pair_dot(h, wo_v, p))
+        h_v[p, far] = h
+        if far == 0:
+            load_wo[p].wait()
+        rs_start(p, far, pair_dot(h, wo_v, p))
 
     def backward_act(p):
-        dyr = wait_rows(1, p)
-        dh = pair_dot(dyr, wo_v, p, ((1,), (1,)))
-        a = act_v[p]
+        wait_rows(1, p, 0)
+        wait_rows(1, p, 1)
+        dh = pair_dot(all_rows(1, p), wo_v, p, ((1,), (1,)))
+        a = act_v[p].reshape(rows, -1)
         a2 = a * a
         th = jnp.tanh(GELU_C * (a + GELU_K * a2 * a))
         slope = 0.5 * (1.0 + th) + 0.5 * a * (1.0 - th * th) * (GELU_C * (1.0 + 3.0 * GELU_K * a2))
         da_v[p] = (dh * slope).astype(BF16)
 
     def backward_in(p):
-        rs_start(2 + p, pair_dot(da_v[p], wi_v, p, ((1,), (1,))))
-
-    def combine(t):
-        halves = [
-            jnp.concatenate([slots_v[2 * t + p, h].reshape(rows, half) for p in range(N_PAIR)], axis=0) for h in (0, 1)
-        ]
-        return dot(onehot_slots[...], jnp.concatenate(halves, axis=1), ((0,), (0,)))
+        part = pair_dot(da_v[p], wi_v, p, ((1,), (1,)))
+        for far in (0, 1):
+            rs_start(2 + p, far, part[far * part_rows : (far + 1) * part_rows])
 
     def weight_grad(n):
         e = n // 2
         p, mask = e // 2, (mask0, mask1)[e % 2]
         if n % 2 == 0:
-            dwo_v[e] = dot(h_v[p] * mask, recv_v[1, p].reshape(rows, d_model), ((0,), (0,)))
+            dwo_v[e] = dot(h_v[p].reshape(rows, -1) * mask, all_rows(1, p), ((0,), (0,)))
         else:
-            dwi_v[e] = dot(recv_v[0, p].reshape(rows, d_model) * mask, da_v[p], ((0,), (0,)))
+            dwi_v[e] = dot(all_rows(0, p) * mask, da_v[p], ((0,), (0,)))
 
     def first(k):
-        step("relay1_", rs_relay, 1, k // 4, k % 4)
+        step("relay1_", rs_relay, 1, *chunks[k])
 
     def second(k):
-        step("relay2_", rs_relay, 2, k // 4, k % 4)
-
-    def last(k):
-        step("final_", rs_final, k // 4, k % 4)
-
-    step("forward", forward, 0)
-    step("forward", forward, 1)
+        step("relay2_", rs_relay, 2, *chunks[k])
+
+    units = [(0, 0), (1, 0), (0, 1), (1, 1), (2, 0), (2, 1), (3, 0), (3, 1)]
+    chunks = [(i, far, b) for i, far in units for b in range(2)]
+
+    step("forward", forward, 0, 0)
+    step("forward", forward, 1, 0)
     first(0)
-    step("bwd_act", backward_act, 0)
+    step("forward", forward, 0, 1)
     first(1)
-    step("bwd_in", backward_in, 0)
     first(2)
     second(0)
-    step("bwd_act", backward_act, 1)
+    step("forward", forward, 1, 1)
     first(3)
     second(1)
+    first(4)
+    step("bwd_act", backward_act, 0)
+    second(2)
+    first(5)
+    step("bwd_in", backward_in, 0)
+    second(3)
+    first(6)
+    step("bwd_act", backward_act, 1)
+    second(4)
+    first(7)
     step("bwd_in", backward_in, 1)
-
-    def back(at, i, pieces=range(N_BACK)):
-        for n in pieces:
-            step(f"ag_fwd{at}_", ag_forward, at, i, n)
-
-    for k in range(4, 16):
+    second(5)
+    for k in range(8, 16):
         first(k)
         second(k - 2)
-        if 6 <= k < 14:
-            step("weight_grad", weight_grad, k - 6)
-    back(2, 0, [0, 1])
+        step("weight_grad", weight_grad, k - 8)
+
+    def turn(i, far):
+        step("back1_", back_first, i, far)
+
+    def back(i, far):
+        step("back2_", back_second, i, far)
+
     second(14)
-    back(2, 0, [2, 3])
+    turn(0, 0)
     second(15)
     for k in range(16):
-        last(k)
-        if k >= 2:
-            step("ag_root", ag_root, (k - 2) // 4, (k - 2) % 4)
-    step("ag_root", ag_root, 3, 2)
-    step("ag_root", ag_root, 3, 3)
-    for n in range(N_BACK):
-        back(2, 1, [n])
-        back(1, 0, [n])
-    for n in range(N_BACK):
-        back(2, 2, [n])
-        back(1, 1, [n])
-    step("ag_last", ag_last, 0)
-    step("ag_last", ag_last, 1)
+        step("final_", rs_final, *chunks[k])
+    for i, far in units[:4]:
+        step("back3_", back_last, i, far)
+    step("hop_", hop_wait, 0)
+    step("hop_", hop_wait, 1)
+    turn(1, 0)
+    turn(0, 1)
+    back(0, 0)
+    turn(1, 1)
+    back(1, 0)
+    turn(2, 0)
+    back(0, 1)
+    turn(2, 1)
+    back(1, 1)
 
     def wg_copy(k):
-        return remote(4, dwg_part, dwg_in.at[k - 1], wg_recv, ep=ep_peer[k])
+        return remote(4, dwg_part, dwg_in.at[k], wg_recv, ep=ep_peer[k])
 
     def finish_y():
-        y_tok = combine(0)
+        y_tok = by_token(0)
         out_v[...] = (gate_v * y_tok).astype(BF16)
         d_gate = jnp.sum(gy_v[...].astype(F32) * y_tok, axis=1, keepdims=True)
         d_gate_row = jnp.transpose(jnp.broadcast_to(d_gate, (n_tok, 128)))[:1]
         d_logits = d_gate_row * router_v[...]
         dwg_part[...] = dot(d_logits.astype(BF16), x_v[...])
-        for k in range(1, N_EP):
+        for k in range(3):
             wg_copy(k).start()
         return dot(jnp.transpose(d_logits).astype(BF16), wg_ref[...])
 
     def finish_wg():
         wait_bytes(dwg_in, wg_recv)
-        dwg_v[...] = (dwg_part[...] + dwg_in[1]) + (dwg_in[0] + dwg_in[2])
+        dwg_v[...] = (dwg_part[...] + dwg_in[0]) + (dwg_in[1] + dwg_in[2])
 
     def finish_s():
-        dx_v[...] = (combine(1) + router_grad).astype(BF16)
+        dx_v[...] = (by_token(1) + router_grad).astype(BF16)
 
     router_grad = step("finish_y", finish_y)
-    for n in range(N_BACK):
-        back(2, 3, [n])
-        back(1, 2, [n])
+    turn(3, 0)
+    back(2, 0)
+    back(2, 1)
+    turn(3, 1)
+    back(3, 0)
+    back(3, 1)
+    for i, far in units[4:]:
+        step("back3_", back_last, i, far)
+    step("hop_", hop_wait, 2)
+    step("hop_", hop_wait, 3)
+    step("finish_s", finish_s)
     step("finish_wg", finish_wg)
-    back(1, 3)
-    step("ag_last", ag_last, 2)
-    step("ag_last", ag_last, 3)
-    step("finish_s", finish_s)
 
     def drain():
         wait_bytes(part_v.at[pl.ds(0, N_EP - 1), 0], sent_sem.at[0])
         wait_bytes(dwg_in, sent_sem.at[4])
 
-        @pl.when((z == 0) | (z == N_TP - 1))
+        @pl.when(at_end)
         def _():
             wait_bytes(part_v.at[:, 0], sent_sem.at[1])
             wait_bytes(red_v.at[:, pl.ds(0, N_EP - 1)], sent_sem.at[2])
-            wait_bytes(slots_v.at[:, 0], sent_sem.at[3])
-
-        @pl.when((z != 0) & (z != N_TP - 1))
+            wait_bytes(red_v, sent_sem.at[5])
+
+        @pl.when(jnp.logical_not(at_end))
         def _():
             wait_bytes(part_v, sent_sem.at[1])
             wait_bytes(slots_v, sent_sem.at[3])
@@ -369,11 +432,12 @@
             pltpu.VMEM(w_in.shape, BF16), pltpu.VMEM(w_out.shape, BF16),
             pltpu.VMEM((2 * rows, n_tok), BF16), pltpu.VMEM((n_exp, n_tok), F32),
             pltpu.VMEM((2, 2, N_EP, block, d_model), BF16), pltpu.VMEM((2, 2, N_EP, block, d_model), BF16),
-            pltpu.VMEM((2, rows, f_loc), F32), pltpu.VMEM((2, rows, f_loc), BF16), pltpu.VMEM((2, rows, f_loc), BF16),
+            pltpu.VMEM((2, 2, rows // 2, f_loc), F32), pltpu.VMEM((2, 2, rows // 2, f_loc), BF16),
+            pltpu.VMEM((2, rows, f_loc), BF16),
             pltpu.VMEM((4, 2, N_EP, block, half), F32), pltpu.VMEM((4, 2, N_EP, block, half), F32),
             pltpu.VMEM((4, N_EP, block, half), BF16), pltpu.VMEM((4, 2, N_EP, block, half), BF16),
             pltpu.VMEM((n_exp, d_model), F32), pltpu.VMEM((3, n_exp, d_model), F32),
-            dma((8,)), dma((5,)), dma((2, 2)), dma((4, 2, N_EP)), dma((4,)), dma((4, 2, N_BACK)), dma,
+            dma((8,)), dma((6,)), dma((2, 2, 2)), dma((4, 2, N_EP)), dma((4, 2)), dma((4, 2)), dma((4, 2)), dma,
         ]
         results = pl.pallas_call(
             functools.partial(moe_kernel, cap),

time: 62.1 us -> 59 us (0.950)
  Pallas kernels: 61.3 us -> 58.2 us
    pallas_call x1, Pallas kernels: 54.6 us -> 51.4 us  [local_block(): pl.pallas_call(functools.partial(moe_kernel, cap), out_shape=held, in_spe...]
where the time goes in v3:
time: 59 us; the launch traced here: 58.9 us
  Pallas kernels  58.2 us (99%)
  between operations  0.64 us (1%)
    pallas_call x1, Pallas kernels, local_block(): pl.pallas_call(functools.partial(moe_kernel, cap), out_shape=held, in_spe...  51.4 us
    pallas_call x1, Pallas kernels, local_block(): pl.pallas_call(store_kernel, out_shape=out_shape, in_specs=[any_spec] * 5...  6.78 us

profile of v3, /device:TPU:0, one launch (start us, length us, event | category | flops | bytes accessed | tf_op | source)
XLA Modules:
  0.0 58.9 jit_solution(13239332048819605349)
XLA Ops:
  0.6 51.4 %shard_map.101 = (bf16[256,768]{1,0:T(8,128)(2,1)S(1)}, bf16[256,768]{1,0:T(8,128)(2,1)S(1)}, f32[16,768]{1,0:T(8,128)S(1)}, f32[4,768,768]{2,1,0:T(8,128)S(1)}, f32[4,768,768]{2,1,0:T(8,128)S(1)}) custom-call(s32[1,256]{1,0:T(1,128)} %bitcast.4, bf16[16,768]{1,0:T(8,128)(2,1)} %bitcast.3, bf16[256,768]{1,0:T(8,128)(2,1)} %x_hbm.1, bf16[256,768]{1,0:T(8,128)(2,1)} %gy_hbm.1, ...), custom_call_target="tpu_custom_call" | custom-call | tf_op jit(solution)/shard_map/pallas_call | solution.py:442
  52.1 6.8 %shard_map.102 = (bf16[256,768]{1,0:T(8,128)(2,1)}, bf16[256,768]{1,0:T(8,128)(2,1)}, f32[16,768]{1,0:T(8,128)}, f32[4,768,768]{2,1,0:T(8,128)}, f32[4,768,768]{2,1,0:T(8,128)}) custom-call(bf16[256,768]{1,0:T(8,128)(2,1)S(1)} %get-tuple-element.15.out_v, bf16[256,768]{1,0:T(8,128)(2,1)S(1)} %get-tuple-element.16.dx_v, ...), custom_call_target="tpu_custom_call" | custom-call | tf_op jit(solution)/shard_map/pallas_call | solution.py:453

commit v4 on v3

v4 whole, which is shorter than its diff:
```python
import functools

import jax
import jax.numpy as jnp
from jax import lax
from jax.experimental import pallas as pl
from jax.experimental.pallas import tpu as pltpu
from jax.sharding import PartitionSpec as P

MESH = pl.DeviceIdType.MESH
F32, BF16 = jnp.float32, jnp.bfloat16
GELU_C = 0.7978845608028654
GELU_K = 0.044715
N_EP, N_TP, N_PAIR = 4, 4, 2


def dot(a, b, dims=((1,), (0,))):
    return lax.dot_general(a, b, (dims, ((), ())), preferred_element_type=F32)


def pair_masks(rows, block, cap):
    row = lax.broadcasted_iota(jnp.int32, (rows, 1), 0)
    first = lax.rem(row, block) < cap
    return jnp.where(first, 1.0, 0.0).astype(BF16), jnp.where(first, 0.0, 1.0).astype(BF16)


def half_by_token(onehot_slots, slots, first, h):
    n, width = onehot_slots.shape[0] // 2, slots.shape[-1]
    return dot(onehot_slots[...], jnp.concatenate([slots[first + p, h].reshape(n, width) for p in range(2)], axis=0), ((0,), (0,)))


def by_token(onehot_slots, slots, first):
    n, width = onehot_slots.shape[0] // 2, slots.shape[-1]
    halves = [jnp.concatenate([slots[first + p, h].reshape(n, width) for p in range(2)], axis=0) for h in (0, 1)]
    return dot(onehot_slots[...], jnp.concatenate(halves, axis=1), ((0,), (0,)))


def moe_kernel(
    cap,
    ids_hbm, wg_hbm, x_hbm, gy_hbm, wi_hbm, wo_hbm,
    gate_v, back_v, onehot_slots, rgrad_v, dwg_v, dwi_v, dwo_v,
    ids_ref, wg_ref, x_v, gy_v, wi_v, wo_v,
    router_v, send_v, recv_v, act_v, h_v, da_v, tmp_v,
    part_v, rs_in, red_v, slots_v,
    dwg_part, dwg_in, gate_rows,
    load_sem, sent_sem, disp_recv, rs_recv, hop_recv, turn_recv, back_recv, last_recv, wg_recv, gate_recv,
):
    block = 2 * cap
    rows = N_EP * block
    n_tok, d_model = x_v.shape
    n_exp = wg_ref.shape[0]
    half = d_model // 2
    z, j = lax.axis_index("tp"), lax.axis_index("ep")
    right, left = lax.rem(z + 1, N_TP), lax.rem(z + N_TP - 1, N_TP)
    chip = j // 2
    near = j + 1 - 2 * lax.rem(j, 2)
    ep_peer = [near, lax.rem(j + 2, N_EP), lax.rem(near + 2, N_EP)]
    side = [2 * chip, 2 - 2 * chip]

    def remote(kind, src, dst, rsem, **dev):
        return pltpu.make_async_remote_copy(
            src_ref=src, dst_ref=dst, send_sem=sent_sem.at[kind], recv_sem=rsem, device_id=dev, device_id_type=MESH
        )

    def wait_bytes(ref, sem):
        pltpu.make_async_copy(ref, ref, sem).wait()

    load_x = pltpu.make_async_copy(x_hbm, x_v, load_sem.at[0])
    load_gy = pltpu.make_async_copy(gy_hbm, gy_v, load_sem.at[1])
    load_wi = [pltpu.make_async_copy(wi_hbm.at[pl.ds(2 * p, 2)], wi_v.at[pl.ds(2 * p, 2)], load_sem.at[2 + p]) for p in range(2)]
    load_wo = [pltpu.make_async_copy(wo_hbm.at[pl.ds(2 * p, 2)], wo_v.at[pl.ds(2 * p, 2)], load_sem.at[4 + p]) for p in range(2)]
    load_ids = pltpu.make_async_copy(ids_hbm, ids_ref, load_sem.at[6])
    load_wg = pltpu.make_async_copy(wg_hbm, wg_ref, load_sem.at[7])
    for load in (load_ids, load_x, load_wg, load_gy):
        load.start()

    barrier = pltpu.get_barrier_semaphore()
    pair_z = z + 1 - 2 * lax.rem(z, 2)
    at_end = (z == 0) | (z == N_TP - 1)

    def greet(**dev):
        pl.semaphore_signal(barrier, inc=1, device_id=dev, device_id_type=MESH)

    for peer in ep_peer:
        greet(ep=peer)
    for peer in [j] + ep_peer:
        greet(tp=pair_z, ep=peer)

    @pl.when(jnp.logical_not(at_end))
    def _():
        greet(tp=N_TP - 1 - z)

    for p in range(2):
        load_wi[p].start()
        load_wo[p].start()

    load_ids.wait()
    ids = ids_ref[...]
    chosen = ids == lax.broadcasted_iota(jnp.int32, (n_exp, n_tok), 0)
    onehot = jnp.where(chosen, 1.0, 0.0)
    before = lax.broadcasted_iota(jnp.int32, (n_tok, n_tok), 0) < lax.broadcasted_iota(jnp.int32, (n_tok, n_tok), 1)
    counts = dot(onehot.astype(BF16), jnp.where(before, 1.0, 0.0).astype(BF16))
    pos = jnp.sum(counts * onehot, axis=0, keepdims=True)
    base = ((ids >> 1) & 1) * rows + (ids >> 2) * block + (ids & 1) * cap
    slot = jnp.where(pos < cap, base.astype(F32) + pos, -1.0)
    slot_iota = lax.broadcasted_iota(jnp.int32, (2 * rows, n_tok), 0).astype(F32)
    onehot_slots[...] = jnp.where(slot_iota == slot, 1.0, 0.0).astype(BF16)

    def dispatch(t, tok_rows):
        packed = dot(onehot_slots[...], tok_rows).astype(BF16)
        send_v[t] = packed.reshape(2, N_EP, block, d_model)

    def disp_copy(t, p, k):
        peer = ep_peer[k]
        return remote(0, send_v.at[t, p, peer], recv_v.at[t, p, j], disp_recv.at[t, p, min(k, 1)], ep=peer)

    def start_dispatch(t):
        for p in range(N_PAIR):
            disp_copy(t, p, 0).start()
        for p in range(N_PAIR):
            for k in (1, 2):
                disp_copy(t, p, k).start()

    def keep_own(t):
        for p in range(N_PAIR):
            recv_v[t, p, j] = send_v[t, p, j]

    def route_x():
        load_x.wait()
        dispatch(0, x_v[...])
        keep_own(0)

    def route_dy():
        load_wg.wait()
        logits = dot(wg_ref[...], x_v[...], ((1,), (1,)))
        expd = jnp.exp(logits - jnp.max(logits, axis=0, keepdims=True))
        prob = expd / jnp.sum(expd, axis=0, keepdims=True)
        gate_row = jnp.sum(jnp.where(chosen, prob, 0.0), axis=0, keepdims=True)
        router_v[...] = prob * (onehot - gate_row)
        gate_all = jnp.transpose(jnp.broadcast_to(gate_row, (128, n_tok)))
        gate_v[...] = gate_all
        gate = gate_all[:, :1]
        load_gy.wait()
        dispatch(1, (gate * gy_v[...].astype(F32)).astype(BF16))

    def meet():
        @pl.when(at_end)
        def _():
            pl.semaphore_wait(barrier, 7)

        @pl.when(jnp.logical_not(at_end))
        def _():
            pl.semaphore_wait(barrier, 8)

    def step(name, f, *a):
        with jax.named_scope(name + "".join(str(v) for v in a if isinstance(v, int))):
            return f(*a)

    mask0, mask1 = pair_masks(rows, block, cap)

    OWN, MATE, NEAR, FAR, ALL = (j, 1), (near, 1), (side[0], 2), (side[1], 2), (0, N_EP)

    def group(ref, p, g):
        return ref[p, pl.ds(*g)].reshape(g[1] * block, ref.shape[-1])

    def put(ref, p, g, value):
        ref[p, pl.ds(*g)] = value.reshape(g[1], block, value.shape[-1])

    def wait_rows(t, p, far):
        wait_bytes(recv_v.at[t, p, pl.ds(0, 1 + far)], disp_recv.at[t, p, far])

    def one_dot(lhs, w_ref, p, which, dims=((1,), (0,))):
        mask = (mask0, mask1)[which]
        return dot(lhs * mask[: lhs.shape[0]], w_ref[2 * p + which], dims)

    def pair_dot(lhs, w_ref, p):
        return one_dot(lhs, w_ref, p, 0) + one_dot(lhs, w_ref, p, 1)

    place = [z, N_TP - 1 - z]
    ahead, behind = [right, left], [left, right]

    def rs_copy(i, h, q):
        return remote(1, part_v.at[i, h, q], rs_in.at[i, h, q], rs_recv.at[i, h, q], tp=ahead[h])

    def rs_start(i, g, part):
        for h in (0, 1):
            part_v[i, h, pl.ds(*g)] = part[:, h * half : (h + 1) * half].reshape(g[1], block, half)
        for h in (0, 1):
            @pl.when(place[h] == 0)
            def _():
                for first, count in (NEAR, FAR) if g is ALL else (g,):
                    for b in range(count):
                        rs_copy(i, h, first + b).start()

    def rs_relay(at, i, q):
        for h in (0, 1):
            @pl.when(place[h] == at)
            def _():
                rs_copy(i, h, q).wait_recv()
                part_v[i, h, q] = part_v[i, h, q] + rs_in[i, h, q]
                rs_copy(i, h, q).start()

    def hop_copy(i, h, q, far):
        return remote(2, red_v.at[i, q], slots_v.at[i, h, j], hop_recv.at[i, far], ep=q)

    def turn_copy(i, h, q, far):
        return remote(5 if i < 3 else 7, red_v.at[i, q], slots_v.at[i, h, j], turn_recv.at[i, far], tp=behind[h], ep=q)

    def last_turn(h, q):
        return remote(7, red_v.at[3, q], slots_v.at[3, h, j], last_recv.at[0, lax.rem(j, 2)], tp=behind[h], ep=q)

    def last_back(h, b):
        part = slots_v.at[3, h, side[1] + b]
        return remote(8, part, part, last_recv.at[1, b], tp=behind[h])

    def last_first(b):
        for h in (0, 1):
            @pl.when(place[h] == 2)
            def _():
                wait_bytes(slots_v.at[3, h, 0], last_recv.at[0, b])
                last_back(h, b).start()

    def last_second(b):
        for h in (0, 1):
            @pl.when(place[h] == 1)
            def _():
                last_back(h, b).wait_recv()
                last_back(h, b).start()

    def last_last(b):
        for h in (0, 1):
            @pl.when(place[h] == 0)
            def _():
                last_back(h, b).wait_recv()

    def turn_start(i, far, q):
        for h in (0, 1):
            @pl.when(place[h] == N_TP - 1)
            def _():
                turn_copy(i, h, q, far).start()

    def sums_sent():
        @pl.when(at_end)
        def _():
            wait_bytes(part_v.at[:, 0], sent_sem.at[1])

    def rs_final(i, far, q, turn=True):
        for h in (0, 1):
            @pl.when(place[h] == N_TP - 1)
            def _():
                rs_copy(i, h, q).wait_recv()
                red_v[i, q] = (part_v[i, h, q] + rs_in[i, h, q]).astype(BF16)
                if (i, far) == (3, 1):
                    last_turn(h, q).start()
                elif turn:
                    turn_copy(i, h, q, far).start()
                if far:
                    hop_copy(i, h, q, far).start()
                else:
                    @pl.when(j != q)
                    def _():
                        hop_copy(i, h, q, far).start()

                    @pl.when(j == q)
                    def _():
                        slots_v[i, h, j] = red_v[i, q]

    def hop_wait(i):
        for far in (0, 1):
            wait_bytes(slots_v.at[i, 0, pl.ds(0, 1 + far)], hop_recv.at[i, far])

    def hop_wait_end(i):
        @pl.when(at_end)
        def _():
            hop_wait(i)

    def back_copy(i, h, far):
        part = slots_v.at[i, h, pl.ds(side[far], 2)]
        return remote(3 if i < 3 else 8, part, part, back_recv.at[i, far], tp=behind[h])

    def back_first(i, far):
        for h in (0, 1):
            @pl.when(place[h] == 2)
            def _():
                wait_bytes(slots_v.at[i, h, pl.ds(0, 2)], turn_recv.at[i, far])
                back_copy(i, h, far).start()

    def back_second(i, far):
        for h in (0, 1):
            @pl.when(place[h] == 1)
            def _():
                back_copy(i, h, far).wait_recv()
                back_copy(i, h, far).start()

    def back_last(i, far):
        for h in (0, 1):
            @pl.when(place[h] == 0)
            def _():
                back_copy(i, h, far).wait_recv()

    def gate_copy(h, at):
        tp = at if h == 0 else N_TP - 1 - at
        return remote(10, gate_rows.at[h], gate_rows.at[h], gate_recv.at[h], tp=tp)

    def gate_root():
        for h in (0, 1):
            @pl.when(place[h] == N_TP - 1)
            def _():
                hop_wait(0)
                hop_wait(1)
                y_tok = half_by_token(onehot_slots, slots_v, 0, h)
                part = jnp.sum(gy_v[:, h * half : (h + 1) * half].astype(F32) * y_tok, axis=1, keepdims=True)
                gate_rows[h] = jnp.transpose(jnp.broadcast_to(part, (n_tok, 128)))[:8]
                for at in range(N_TP - 1):
                    gate_copy(h, at).start()

    def wg_copy(k):
        return remote(4, dwg_part, dwg_in.at[k], wg_recv, ep=ep_peer[k])

    def router_back():
        for h in (0, 1):
            @pl.when(place[h] != N_TP - 1)
            def _():
                gate_copy(h, 0).wait_recv()
        d_logits = (gate_rows[0, :1] + gate_rows[1, :1]) * router_v[...]
        dwg_part[...] = dot(d_logits.astype(BF16), x_v[...])
        for k in range(3):
            wg_copy(k).start()
        rgrad_v[...] = dot(jnp.transpose(d_logits).astype(BF16), wg_ref[...])

    def forward_act(p, g):
        a = pair_dot(group(recv_v.at[0], p, g), wi_v, p)
        put(act_v, p, g, a)
        put(h_v, p, g, (0.5 * a * (1.0 + jnp.tanh(GELU_C * (a + GELU_K * a * a * a)))).astype(BF16))

    def forward_out(p, g):
        rs_start(p, g, pair_dot(group(h_v, p, g), wo_v, p))

    NT = ((1,), (1,))

    def backward_act0(p, g):
        put(tmp_v, 0, g, one_dot(group(recv_v.at[1], p, g), wo_v, p, 0, NT))

    def backward_act1(p, g):
        dh = group(tmp_v, 0, g) + one_dot(group(recv_v.at[1], p, g), wo_v, p, 1, NT)
        a = group(act_v, p, g)
        a2 = a * a
        th = jnp.tanh(GELU_C * (a + GELU_K * a2 * a))
        slope = 0.5 * (1.0 + th) + 0.5 * a * (1.0 - th * th) * (GELU_C * (1.0 + 3.0 * GELU_K * a2))
        put(da_v, p, g, (dh * slope).astype(BF16))

    def backward_in0(p, g):
        put(tmp_v, 1, g, one_dot(group(da_v, p, g), wi_v, p, 0, NT))

    def backward_in1(p, g):
        rs_start(2 + p, g, group(tmp_v, 1, g) + one_dot(group(da_v, p, g), wi_v, p, 1, NT))

    def weight_grad(n):
        e = n // 2
        p, mask = e // 2, (mask0, mask1)[e % 2]
        if n % 2 == 0:
            dwo_v[e] = dot(group(h_v, p, ALL) * mask, group(recv_v.at[1], p, ALL), ((0,), (0,)))
        else:
            dwi_v[e] = dot(group(recv_v.at[0], p, ALL) * mask, group(da_v, p, ALL), ((0,), (0,)))

    order = [(0, 0, OWN), (0, 0, MATE), (1, 0, NEAR), (2, 0, NEAR), (0, 1, FAR), (1, 1, FAR), (2, 1, FAR), (3, 0, NEAR), (3, 1, FAR)]
    chunks = [(i, far, g[0] + b) for i, far, g in order for b in range(g[1])]

    def relay(at, k):
        with jax.named_scope(f"relay{at}_{k}"):
            rs_relay(at, chunks[k][0], chunks[k][2])

    def wait_both(t, p):
        wait_rows(t, p, 0)
        wait_rows(t, p, 1)

    def own_act():
        load_wi[0].wait()
        forward_act(0, OWN)

    def own_out():
        load_wo[0].wait()
        forward_out(0, OWN)

    def start_mate():
        wait_rows(0, 0, 0)
        forward_act(0, MATE)
        forward_out(0, MATE)

    def near_next():
        load_wi[1].wait()
        wait_rows(0, 1, 0)
        forward_act(1, NEAR)

    def near_next_out():
        load_wo[1].wait()
        forward_out(1, NEAR)

    def back_units(p, g, wait):
        def head():
            wait()
            backward_act0(p, g)

        return [head] + [functools.partial(f, p, g) for f in (backward_act1, backward_in0, backward_in1)]

    def far_units(p):
        def head():
            wait_rows(0, p, 1)
            forward_act(p, FAR)

        return [head, functools.partial(forward_out, p, FAR)]

    step("route_x", route_x)
    step("meet", meet)
    start_dispatch(0)
    step("own_act", own_act)
    step("own_out", own_out)
    step("mate", start_mate)
    step("route_dy", route_dy)
    keep_own(1)
    start_dispatch(1)
    step("near1", near_next)
    step("near1_out", near_next_out)

    def timed(ready, lengths, units):
        return [(ready, length, f) for length, f in zip(lengths, units)]

    work = timed(7.0, (0.42, 0.62, 0.42, 0.62), back_units(0, NEAR, lambda: wait_rows(1, 0, 0)))
    work += timed(7.9, (0.62, 0.62), far_units(0)) + timed(11.0, (0.62, 0.62), far_units(1))
    work += timed(13.5, (0.42, 0.6, 0.42, 0.6), back_units(0, FAR, lambda: wait_rows(1, 0, 1)))
    work += timed(16.5, (0.47, 0.65, 0.47, 0.65), back_units(1, ALL, lambda: wait_both(1, 1)))
    work += timed(16.5, (0.61,) * 8, [functools.partial(weight_grad, n) for n in range(8)])
    relays = [(7.0 + 1.31 * k, 1, k) for k in range(16)] + [(10.4 + 1.31 * k, 2, k) for k in range(16)]
    relays = sorted(relays)[:-2]
    now, n_work = 7.2, 0
    while relays or work:
        due = relays[0][0] if relays else 1e9
        ready = work[0][0] if work else 1e9
        if work and ready <= now and (now + work[0][1] <= due + 0.15):
            step(f"work{n_work}", work[0][2])
            now += work.pop(0)[1]
            n_work += 1
        elif relays and due <= max(now, ready):
            relay(*relays.pop(0)[1:])
            now = max(now, due) + 0.1
        else:
            now = min(due, max(now, ready)) if ready > now else due

    def turn(i, far):
        step("back1_", back_first, i, far)

    def back(i, far):
        step("back2_", back_second, i, far)

    pieces = [(0, 0), (1, 0), (2, 0), (0, 1), (1, 1), (2, 1), (3, 0)]
    turn(*pieces[0])
    relay(2, 14)
    turn(*pieces[1])
    relay(2, 15)
    for k in range(16):
        step(f"final{k}_", rs_final, *chunks[k], k >= 6)
        if k == 5:
            step("sums_sent", sums_sent)
            for n in range(6):
                turn_start(*chunks[n])
        if k == 12:
            step("gate_root", gate_root)
    def finish_wg():
        wait_bytes(dwg_in, wg_recv)
        dwg_v[...] = (dwg_part[...] + dwg_in[0]) + (dwg_in[1] + dwg_in[2])

    def hand_over():
        back_v[...] = slots_v[...]

    for n in range(2, 7):
        turn(*pieces[n])
        back(*pieces[n - 2])
        if n == 5:
            step("router_back", router_back)
    back(*pieces[5])
    step("last_first", last_first, 0)
    step("last_first", last_first, 1)
    back(*pieces[6])
    step("last_second", last_second, 0)
    step("last_second", last_second, 1)
    for n in range(7):
        step("back3_", back_last, *pieces[n])
    step("last_last", last_last, 0)
    step("last_last", last_last, 1)
    step("hop_", hop_wait_end, 2)
    step("hop_", hop_wait_end, 3)
    step("hand_over", hand_over)
    step("finish_wg", finish_wg)

    def drain():
        wait_bytes(part_v.at[pl.ds(0, N_EP - 1), 0], sent_sem.at[0])
        wait_bytes(dwg_in, sent_sem.at[4])

        @pl.when(at_end)
        def _():
            wait_bytes(red_v.at[:, pl.ds(0, N_EP - 1)], sent_sem.at[2])
            wait_bytes(red_v.at[pl.ds(0, 3)], sent_sem.at[5])
            wait_bytes(red_v.at[0], sent_sem.at[7])
            wait_bytes(gate_rows.at[pl.ds(0, 3)], sent_sem.at[10])

        @pl.when(jnp.logical_not(at_end))
        def _():
            wait_bytes(part_v, sent_sem.at[1])
            wait_bytes(slots_v.at[pl.ds(0, 3)], sent_sem.at[3])
            wait_bytes(slots_v.at[0], sent_sem.at[8])

    step("drain", drain)


def store_kernel(
    gate_v, back_v, onehot_slots, rgrad_v, dwg_v, dwi_v, dwo_v, out_hbm, dx_hbm, dwg_hbm, dwi_hbm, dwo_hbm, out_v, dx_v, sem
):
    pairs = [(dwi_v.at[e], dwi_hbm.at[e]) for e in range(4)] + [(dwo_v.at[e], dwo_hbm.at[e]) for e in range(4)]
    pairs += [(dwg_v, dwg_hbm), (out_v, out_hbm), (dx_v, dx_hbm)]
    copies = [pltpu.make_async_copy(src, dst, sem.at[n]) for n, (src, dst) in enumerate(pairs)]
    for cp in copies[:-2]:
        cp.start()
    out_v[...] = (gate_v[:, :1] * by_token(onehot_slots, back_v, 0)).astype(BF16)
    copies[-2].start()
    dx_v[...] = (by_token(onehot_slots, back_v, 2) + rgrad_v[...]).astype(BF16)
    copies[-1].start()
    for cp in copies:
        cp.wait()


def solution(mesh):
    row_spec = P(("dp", "ep"), None)

    def local_block(tokens, grad_out, w_router, w_in, w_out, expert_ids):
        n_tok, d_model = tokens.shape
        n_exp = w_router.shape[1]
        n_loc, _, f_loc = w_in.shape
        cap = (6 * n_tok + 5 * n_exp - 1) // (5 * n_exp)
        block, rows, half = 2 * cap, 8 * cap, d_model // 2
        S = jax.ShapeDtypeStruct
        any_spec, vmem_spec = pl.BlockSpec(memory_space=pl.ANY), pl.BlockSpec(memory_space=pltpu.VMEM)
        dma = pltpu.SemaphoreType.DMA
        out_shape = (
            S((n_tok, d_model), BF16), S((n_tok, d_model), BF16), S((n_exp, d_model), F32),
            S((n_loc, d_model, f_loc), F32), S((n_loc, f_loc, d_model), F32),
        )
        handed = (
            S((n_tok, 128), F32), S((4, 2, N_EP, block, half), BF16), S((2 * rows, n_tok), BF16), S((n_tok, d_model), F32),
        ) + out_shape[2:]
        held = tuple(pltpu.VMEM(s.shape, s.dtype) for s in handed)
        scratch = [
            pltpu.VMEM((1, n_tok), jnp.int32), pltpu.VMEM((n_exp, d_model), BF16),
            pltpu.VMEM((n_tok, d_model), BF16), pltpu.VMEM((n_tok, d_model), BF16),
            pltpu.VMEM(w_in.shape, BF16), pltpu.VMEM(w_out.shape, BF16),
            pltpu.VMEM((n_exp, n_tok), F32),
            pltpu.VMEM((2, 2, N_EP, block, d_model), BF16), pltpu.VMEM((2, 2, N_EP, block, d_model), BF16),
            pltpu.VMEM((2, N_EP, block, f_loc), F32), pltpu.VMEM((2, N_EP, block, f_loc), BF16),
            pltpu.VMEM((2, N_EP, block, f_loc), BF16), pltpu.VMEM((2, N_EP, block, d_model), F32),
            pltpu.VMEM((4, 2, N_EP, block, half), F32), pltpu.VMEM((4, 2, N_EP, block, half), F32),
            pltpu.VMEM((4, N_EP, block, half), BF16), pltpu.VMEM((4, 2, N_EP, block, half), BF16),
            pltpu.VMEM((n_exp, d_model), F32), pltpu.VMEM((3, n_exp, d_model), F32), pltpu.VMEM((4, 8, n_tok), F32),
            dma((8,)), dma((11,)), dma((2, 2, 2)), dma((4, 2, N_EP)), dma((4, 2)), dma((4, 2)), dma((4, 2)), dma((2, 2)), dma, dma((2,)),
        ]
        results = pl.pallas_call(
            functools.partial(moe_kernel, cap),
            out_shape=held,
            in_specs=[any_spec] * 6,
            out_specs=(vmem_spec,) * 7,
            scratch_shapes=scratch,
            compiler_params=pltpu.CompilerParams(collective_id=0, has_side_effects=True, vmem_limit_bytes=24 * 2**20),
        )(*[
            pltpu.with_memory_space_constraint(r, pltpu.HBM)
            for r in (expert_ids.reshape(1, n_tok), w_router.T, tokens, grad_out, w_in, w_out)
        ])
        out, dx, dwg, dwi, dwo = pl.pallas_call(
            store_kernel,
            out_shape=out_shape,
            in_specs=[vmem_spec] * 7,
            out_specs=(any_spec,) * 5,
            scratch_shapes=[pltpu.VMEM((n_tok, d_model), BF16), pltpu.VMEM((n_tok, d_model), BF16), dma((11,))],
            compiler_params=pltpu.CompilerParams(vmem_limit_bytes=8 * 2**20),
        )(*[pltpu.with_memory_space_constraint(r, pltpu.VMEM) for r in results])
        return out, dx, dwi, dwo, dwg.T

    in_specs = (row_spec, row_spec, P(None, None), P("ep", None, "tp"), P("ep", "tp", None), P(("dp", "ep")))
    out_specs = (row_spec, row_spec, P(("dp", "ep"), None, "tp"), P(("dp", "ep"), "tp", None), P("dp", None))
    return jax.shard_map(local_block, mesh=mesh, in_specs=in_specs, out_specs=out_specs, check_vma=False)
```

time: 59 us -> 57.8 us (0.980)
  Pallas kernels: 58.2 us -> 56.8 us
    pallas_call x1, Pallas kernels: 51.4 us -> 50 us  [local_block(): pl.pallas_call(functools.partial(moe_kernel, cap), out_shape=held, in_spe...]
where the time goes in v4:
time: 57.8 us; the launch traced here: 57.6 us
  Pallas kernels  56.8 us (98%)
  between operations  0.8 us (1%)
    pallas_call x1, Pallas kernels, local_block(): pl.pallas_call(functools.partial(moe_kernel, cap), out_shape=held, in_spe...  50 us
    pallas_call x1, Pallas kernels, local_block(): pl.pallas_call(store_kernel, out_shape=out_shape, in_specs=[vmem_spec] *...  6.79 us

profile of v4, /device:TPU:0, one launch (start us, length us, event | category | flops | bytes accessed | tf_op | source)
XLA Modules:
  0.0 57.6 jit_solution(4889417532804997683)
XLA Ops:
  0.6 50.0 %shard_map.101 = (f32[256,128]{1,0:T(8,128)S(1)}, bf16[4,2,4,40,384]{4,3,2,1,0:T(8,128)(2,1)S(1)}, bf16[320,256]{1,0:T(8,128)(2,1)S(1)}, f32[256,768]{1,0:T(8,12...) custom-call(s32[1,256]{1,0:T(1,128)} %bitcast.4, bf16[16,768]{1,0:T(8,128)(2,1)} %bitcast.3, ...), custom_call_target="tpu_custom_call" | custom-call | tf_op jit(solution)/shard_map/pallas_call | solution.py:564
  50.7 6.8 %shard_map.102 = (bf16[256,768]{1,0:T(8,128)(2,1)}, bf16[256,768]{1,0:T(8,128)(2,1)}, f32[16,768]{1,0:T(8,128)}, f32[4,768,768]{2,1,0:T(8,128)}, f32[4,768,768]{2,1,0:T(8,128)}) custom-call(f32[256,128]{1,0:T(8,128)S(1)} %get-tuple-element.17.gate_v, bf16[4,2,4,40,384]{4,3,2,1,0:T(8,128)(2,1)S(1)} %get-tuple-element.18.back_v, ...), custom_call_target="tpu_custom_call" | custom-call | tf_op jit(solution)/shard_map/pallas_call | solution.py:575

commit v5 on v4

--- a/solution.py
+++ b/solution.py
@@ -12,6 +12,7 @@
 GELU_C = 0.7978845608028654
 GELU_K = 0.044715
 N_EP, N_TP, N_PAIR = 4, 4, 2
+HALVES = range(2)
 
 
 def dot(a, b, dims=((1,), (0,))):
@@ -31,7 +32,7 @@
 
 def by_token(onehot_slots, slots, first):
     n, width = onehot_slots.shape[0] // 2, slots.shape[-1]
-    halves = [jnp.concatenate([slots[first + p, h].reshape(n, width) for p in range(2)], axis=0) for h in (0, 1)]
+    halves = [jnp.concatenate([slots[first + p, h].reshape(n, width) for p in range(2)], axis=0) for h in HALVES]
     return dot(onehot_slots[...], jnp.concatenate(halves, axis=1), ((0,), (0,)))
 
 
@@ -71,7 +72,7 @@
     load_wo = [pltpu.make_async_copy(wo_hbm.at[pl.ds(2 * p, 2)], wo_v.at[pl.ds(2 * p, 2)], load_sem.at[4 + p]) for p in range(2)]
     load_ids = pltpu.make_async_copy(ids_hbm, ids_ref, load_sem.at[6])
     load_wg = pltpu.make_async_copy(wg_hbm, wg_ref, load_sem.at[7])
-    for load in (load_ids, load_x, load_wg, load_gy):
+    for load in (load_ids, load_x, load_wi[0], load_wo[0], load_wg, load_gy, load_wi[1], load_wo[1]):
         load.start()
 
     barrier = pltpu.get_barrier_semaphore()
@@ -89,10 +90,6 @@
     @pl.when(jnp.logical_not(at_end))
     def _():
         greet(tp=N_TP - 1 - z)
-
-    for p in range(2):
-        load_wi[p].start()
-        load_wo[p].start()
 
     load_ids.wait()
     ids = ids_ref[...]
@@ -183,9 +180,9 @@
         return remote(1, part_v.at[i, h, q], rs_in.at[i, h, q], rs_recv.at[i, h, q], tp=ahead[h])
 
     def rs_start(i, g, part):
-        for h in (0, 1):
+        for h in HALVES:
             part_v[i, h, pl.ds(*g)] = part[:, h * half : (h + 1) * half].reshape(g[1], block, half)
-        for h in (0, 1):
+        for h in HALVES:
             @pl.when(place[h] == 0)
             def _():
                 for first, count in (NEAR, FAR) if g is ALL else (g,):
@@ -193,7 +190,7 @@
                         rs_copy(i, h, first + b).start()
 
     def rs_relay(at, i, q):
-        for h in (0, 1):
+        for h in HALVES:
             @pl.when(place[h] == at)
             def _():
                 rs_copy(i, h, q).wait_recv()
@@ -214,45 +211,34 @@
         return remote(8, part, part, last_recv.at[1, b], tp=behind[h])
 
     def last_first(b):
-        for h in (0, 1):
+        for h in HALVES:
             @pl.when(place[h] == 2)
             def _():
                 wait_bytes(slots_v.at[3, h, 0], last_recv.at[0, b])
                 last_back(h, b).start()
 
     def last_second(b):
-        for h in (0, 1):
+        for h in HALVES:
             @pl.when(place[h] == 1)
             def _():
                 last_back(h, b).wait_recv()
                 last_back(h, b).start()
 
     def last_last(b):
-        for h in (0, 1):
+        for h in HALVES:
             @pl.when(place[h] == 0)
             def _():
                 last_back(h, b).wait_recv()
 
-    def turn_start(i, far, q):
-        for h in (0, 1):
-            @pl.when(place[h] == N_TP - 1)
-            def _():
-                turn_copy(i, h, q, far).start()
-
-    def sums_sent():
-        @pl.when(at_end)
-        def _():
-            wait_bytes(part_v.at[:, 0], sent_sem.at[1])
-
-    def rs_final(i, far, q, turn=True):
-        for h in (0, 1):
+    def rs_final(i, far, q):
+        for h in HALVES:
             @pl.when(place[h] == N_TP - 1)
             def _():
                 rs_copy(i, h, q).wait_recv()
                 red_v[i, q] = (part_v[i, h, q] + rs_in[i, h, q]).astype(BF16)
                 if (i, far) == (3, 1):
                     last_turn(h, q).start()
-                elif turn:
+                else:
                     turn_copy(i, h, q, far).start()
                 if far:
                     hop_copy(i, h, q, far).start()
@@ -266,7 +252,7 @@
                         slots_v[i, h, j] = red_v[i, q]
 
     def hop_wait(i):
-        for far in (0, 1):
+        for far in HALVES:
             wait_bytes(slots_v.at[i, 0, pl.ds(0, 1 + far)], hop_recv.at[i, far])
 
     def hop_wait_end(i):
@@ -279,21 +265,21 @@
         return remote(3 if i < 3 else 8, part, part, back_recv.at[i, far], tp=behind[h])
 
     def back_first(i, far):
-        for h in (0, 1):
+        for h in HALVES:
             @pl.when(place[h] == 2)
             def _():
                 wait_bytes(slots_v.at[i, h, pl.ds(0, 2)], turn_recv.at[i, far])
                 back_copy(i, h, far).start()
 
     def back_second(i, far):
-        for h in (0, 1):
+        for h in HALVES:
             @pl.when(place[h] == 1)
             def _():
                 back_copy(i, h, far).wait_recv()
                 back_copy(i, h, far).start()
 
     def back_last(i, far):
-        for h in (0, 1):
+        for h in HALVES:
             @pl.when(place[h] == 0)
             def _():
                 back_copy(i, h, far).wait_recv()
@@ -303,7 +289,7 @@
         return remote(10, gate_rows.at[h], gate_rows.at[h], gate_recv.at[h], tp=tp)
 
     def gate_root():
-        for h in (0, 1):
+        for h in HALVES:
             @pl.when(place[h] == N_TP - 1)
             def _():
                 hop_wait(0)
@@ -318,7 +304,7 @@
         return remote(4, dwg_part, dwg_in.at[k], wg_recv, ep=ep_peer[k])
 
     def router_back():
-        for h in (0, 1):
+        for h in HALVES:
             @pl.when(place[h] != N_TP - 1)
             def _():
                 gate_copy(h, 0).wait_recv()
@@ -366,9 +352,14 @@
     order = [(0, 0, OWN), (0, 0, MATE), (1, 0, NEAR), (2, 0, NEAR), (0, 1, FAR), (1, 1, FAR), (2, 1, FAR), (3, 0, NEAR), (3, 1, FAR)]
     chunks = [(i, far, g[0] + b) for i, far, g in order for b in range(g[1])]
 
+    pieces = [(0, 0), (1, 0), (2, 0), (0, 1), (1, 1), (2, 1), (3, 0)]
+
     def relay(at, k):
         with jax.named_scope(f"relay{at}_{k}"):
-            rs_relay(at, chunks[k][0], chunks[k][2])
+            if at == 3:
+                back_first(*pieces[k])
+            else:
+                rs_relay(at, chunks[k][0], chunks[k][2])
 
     def wait_both(t, p):
         wait_rows(t, p, 0)
@@ -430,8 +421,8 @@
     work += timed(13.5, (0.42, 0.6, 0.42, 0.6), back_units(0, FAR, lambda: wait_rows(1, 0, 1)))
     work += timed(16.5, (0.47, 0.65, 0.47, 0.65), back_units(1, ALL, lambda: wait_both(1, 1)))
     work += timed(16.5, (0.61,) * 8, [functools.partial(weight_grad, n) for n in range(8)])
-    relays = [(7.0 + 1.31 * k, 1, k) for k in range(16)] + [(10.4 + 1.31 * k, 2, k) for k in range(16)]
-    relays = sorted(relays)[:-2]
+    relays = [(7.0 + 1.33 * k, 1, k) for k in range(16)] + [(11.4 + 1.33 * k, 2, k) for k in range(16)]
+    relays = sorted(relays + [(28.4 + 1.31 * k, 3, k) for k in range(3)])
     now, n_work = 7.2, 0
     while relays or work:
         due = relays[0][0] if relays else 1e9
@@ -452,17 +443,8 @@
     def back(i, far):
         step("back2_", back_second, i, far)
 
-    pieces = [(0, 0), (1, 0), (2, 0), (0, 1), (1, 1), (2, 1), (3, 0)]
-    turn(*pieces[0])
-    relay(2, 14)
-    turn(*pieces[1])
-    relay(2, 15)
     for k in range(16):
-        step(f"final{k}_", rs_final, *chunks[k], k >= 6)
-        if k == 5:
-            step("sums_sent", sums_sent)
-            for n in range(6):
-                turn_start(*chunks[n])
+        step(f"final{k}_", rs_final, *chunks[k])
         if k == 12:
             step("gate_root", gate_root)
     def finish_wg():
@@ -473,7 +455,8 @@
         back_v[...] = slots_v[...]
 
     for n in range(2, 7):
-        turn(*pieces[n])
+        if n > 2:
+            turn(*pieces[n])
         back(*pieces[n - 2])
         if n == 5:
             step("router_back", router_back)
@@ -498,6 +481,7 @@
 
         @pl.when(at_end)
         def _():
+            wait_bytes(part_v.at[:, 0], sent_sem.at[1])
             wait_bytes(red_v.at[:, pl.ds(0, N_EP - 1)], sent_sem.at[2])
             wait_bytes(red_v.at[pl.ds(0, 3)], sent_sem.at[5])
             wait_bytes(red_v.at[0], sent_sem.at[7])

time: 57.8 us -> 57.1 us (0.988)
  Pallas kernels: 56.8 us -> 56.1 us
    pallas_call x1, Pallas kernels: 50 us -> 49.3 us  [local_block(): pl.pallas_call(functools.partial(moe_kernel, cap), out_shape=held, in_spe...]
where the time goes in v5:
time: 57.1 us; the launch traced here: 56.9 us
  Pallas kernels  56.1 us (98%)
  between operations  0.8 us (1%)
    pallas_call x1, Pallas kernels, local_block(): pl.pallas_call(functools.partial(moe_kernel, cap), out_shape=held, in_spe...  49.3 us
    pallas_call x1, Pallas kernels, local_block(): pl.pallas_call(store_kernel, out_shape=out_shape, in_specs=[vmem_spec] *...  6.79 us

profile of v5, /device:TPU:0, one launch (start us, length us, event | category | flops | bytes accessed | tf_op | source)
XLA Modules:
  0.0 56.9 jit_solution(7112091349434402660)
XLA Ops:
  0.6 49.3 %shard_map.101 = (f32[256,128]{1,0:T(8,128)S(1)}, bf16[4,2,4,40,384]{4,3,2,1,0:T(8,128)(2,1)S(1)}, bf16[320,256]{1,0:T(8,128)(2,1)S(1)}, f32[256,768]{1,0:T(8,12...) custom-call(s32[1,256]{1,0:T(1,128)} %bitcast.4, bf16[16,768]{1,0:T(8,128)(2,1)} %bitcast.3, ...), custom_call_target="tpu_custom_call" | custom-call | tf_op jit(solution)/shard_map/pallas_call | solution.py:548
  49.9 6.8 %shard_map.102 = (bf16[256,768]{1,0:T(8,128)(2,1)}, bf16[256,768]{1,0:T(8,128)(2,1)}, f32[16,768]{1,0:T(8,128)}, f32[4,768,768]{2,1,0:T(8,128)}, f32[4,768,768]{2,1,0:T(8,128)}) custom-call(f32[256,128]{1,0:T(8,128)S(1)} %get-tuple-element.17.gate_v, bf16[4,2,4,40,384]{4,3,2,1,0:T(8,128)(2,1)S(1)} %get-tuple-element.18.back_v, ...), custom_call_target="tpu_custom_call" | custom-call | tf_op jit(solution)/shard_map/pallas_call | solution.py:559

commit v6 on v5

--- a/solution.py
+++ b/solution.py
@@ -13,6 +13,7 @@
 GELU_K = 0.044715
 N_EP, N_TP, N_PAIR = 4, 4, 2
 HALVES = range(2)
+LAST = 3
 
 
 def dot(a, b, dims=((1,), (0,))):
@@ -68,11 +69,14 @@
 
     load_x = pltpu.make_async_copy(x_hbm, x_v, load_sem.at[0])
     load_gy = pltpu.make_async_copy(gy_hbm, gy_v, load_sem.at[1])
-    load_wi = [pltpu.make_async_copy(wi_hbm.at[pl.ds(2 * p, 2)], wi_v.at[pl.ds(2 * p, 2)], load_sem.at[2 + p]) for p in range(2)]
-    load_wo = [pltpu.make_async_copy(wo_hbm.at[pl.ds(2 * p, 2)], wo_v.at[pl.ds(2 * p, 2)], load_sem.at[4 + p]) for p in range(2)]
+    def load_weights(src, dst, first, count, n):
+        return pltpu.make_async_copy(src.at[pl.ds(first, count)], dst.at[pl.ds(first, count)], load_sem.at[n])
+
+    load_wi = [load_weights(wi_hbm, wi_v, *a) for a in ((0, 1, 2), (1, 1, 3), (2, 2, 4))]
+    load_wo = [load_weights(wo_hbm, wo_v, *a) for a in ((0, 1, 8), (1, 1, 9), (2, 2, 5))]
     load_ids = pltpu.make_async_copy(ids_hbm, ids_ref, load_sem.at[6])
     load_wg = pltpu.make_async_copy(wg_hbm, wg_ref, load_sem.at[7])
-    for load in (load_ids, load_x, load_wi[0], load_wo[0], load_wg, load_gy, load_wi[1], load_wo[1]):
+    for load in (load_ids, load_x, *load_wi[:2], *load_wo[:2], load_wg, load_gy, load_wi[2], load_wo[2]):
         load.start()
 
     barrier = pltpu.get_barrier_semaphore()
@@ -170,14 +174,26 @@
         mask = (mask0, mask1)[which]
         return dot(lhs * mask[: lhs.shape[0]], w_ref[2 * p + which], dims)
 
-    def pair_dot(lhs, w_ref, p):
-        return one_dot(lhs, w_ref, p, 0) + one_dot(lhs, w_ref, p, 1)
+    def pair_dot(lhs, w_ref, p, *loads):
+        terms = []
+        for which in HALVES:
+            if loads:
+                loads[which].wait()
+            terms.append(one_dot(lhs, w_ref, p, which))
+        return terms[0] + terms[1]
 
     place = [z, N_TP - 1 - z]
     ahead, behind = [right, left], [left, right]
 
-    def rs_copy(i, h, q):
-        return remote(1, part_v.at[i, h, q], rs_in.at[i, h, q], rs_recv.at[i, h, q], tp=ahead[h])
+    cut = block // 16 * 8 + 8
+    parts = [pl.ds(0, cut), pl.ds(cut, block - cut)]
+
+    def rows_of(i, part):
+        return parts[part] if i == LAST else slice(None)
+
+    def rs_copy(i, h, q, part):
+        where = rows_of(i, part)
+        return remote(1, part_v.at[i, h, q, where], rs_in.at[i, h, q, where], rs_recv.at[i + part, h, q], tp=ahead[h])
 
     def rs_start(i, g, part):
         for h in HALVES:
@@ -187,57 +203,62 @@
             def _():
                 for first, count in (NEAR, FAR) if g is ALL else (g,):
                     for b in range(count):
-                        rs_copy(i, h, first + b).start()
-
-    def rs_relay(at, i, q):
+                        for n in HALVES if i == LAST else range(1):
+                            rs_copy(i, h, first + b, n).start()
+
+    def rs_relay(at, i, far, q, part):
+        where = rows_of(i, part)
         for h in HALVES:
             @pl.when(place[h] == at)
             def _():
-                rs_copy(i, h, q).wait_recv()
-                part_v[i, h, q] = part_v[i, h, q] + rs_in[i, h, q]
-                rs_copy(i, h, q).start()
+                rs_copy(i, h, q, part).wait_recv()
+                part_v[i, h, q, where] = part_v[i, h, q, where] + rs_in[i, h, q, where]
+                rs_copy(i, h, q, part).start()
 
     def hop_copy(i, h, q, far):
         return remote(2, red_v.at[i, q], slots_v.at[i, h, j], hop_recv.at[i, far], ep=q)
 
     def turn_copy(i, h, q, far):
-        return remote(5 if i < 3 else 7, red_v.at[i, q], slots_v.at[i, h, j], turn_recv.at[i, far], tp=behind[h], ep=q)
-
-    def last_turn(h, q):
-        return remote(7, red_v.at[3, q], slots_v.at[3, h, j], last_recv.at[0, lax.rem(j, 2)], tp=behind[h], ep=q)
-
-    def last_back(h, b):
-        part = slots_v.at[3, h, side[1] + b]
-        return remote(8, part, part, last_recv.at[1, b], tp=behind[h])
-
-    def last_first(b):
+        return remote(5, red_v.at[i, q], slots_v.at[i, h, j], turn_recv.at[i, far], tp=behind[h], ep=q)
+
+    def last_turn(h, q, far):
+        return remote(7, red_v.at[LAST, q], slots_v.at[LAST, h, j], last_recv.at[0, far, lax.rem(j, 2)], tp=behind[h], ep=q)
+
+    def last_back(h, far, b):
+        part = slots_v.at[LAST, h, side[far] + b]
+        return remote(8, part, part, last_recv.at[1, far, b], tp=behind[h])
+
+    def last_first(far, b):
         for h in HALVES:
             @pl.when(place[h] == 2)
             def _():
-                wait_bytes(slots_v.at[3, h, 0], last_recv.at[0, b])
-                last_back(h, b).start()
-
-    def last_second(b):
+                wait_bytes(slots_v.at[LAST, h, 0], last_recv.at[0, far, b])
+                last_back(h, far, b).start()
+
+    def last_second(far, b):
         for h in HALVES:
             @pl.when(place[h] == 1)
             def _():
-                last_back(h, b).wait_recv()
-                last_back(h, b).start()
-
-    def last_last(b):
+                last_back(h, far, b).wait_recv()
+                last_back(h, far, b).start()
+
+    def last_last(far, b):
         for h in HALVES:
             @pl.when(place[h] == 0)
             def _():
-                last_back(h, b).wait_recv()
-
-    def rs_final(i, far, q):
+                last_back(h, far, b).wait_recv()
+
+    def rs_final(i, far, q, part):
+        where = rows_of(i, part)
         for h in HALVES:
             @pl.when(place[h] == N_TP - 1)
             def _():
-                rs_copy(i, h, q).wait_recv()
-                red_v[i, q] = (part_v[i, h, q] + rs_in[i, h, q]).astype(BF16)
-                if (i, far) == (3, 1):
-                    last_turn(h, q).start()
+                rs_copy(i, h, q, part).wait_recv()
+                red_v[i, q, where] = (part_v[i, h, q, where] + rs_in[i, h, q, where]).astype(BF16)
+                if i == LAST and part == 0:
+                    return
+                if i == LAST:
+                    last_turn(h, q, far).start()
                 else:
                     turn_copy(i, h, q, far).start()
                 if far:
@@ -262,7 +283,7 @@
 
     def back_copy(i, h, far):
         part = slots_v.at[i, h, pl.ds(side[far], 2)]
-        return remote(3 if i < 3 else 8, part, part, back_recv.at[i, far], tp=behind[h])
+        return remote(3, part, part, back_recv.at[i, far], tp=behind[h])
 
     def back_first(i, far):
         for h in HALVES:
@@ -314,13 +335,13 @@
             wg_copy(k).start()
         rgrad_v[...] = dot(jnp.transpose(d_logits).astype(BF16), wg_ref[...])
 
-    def forward_act(p, g):
-        a = pair_dot(group(recv_v.at[0], p, g), wi_v, p)
+    def forward_act(p, g, *loads):
+        a = pair_dot(group(recv_v.at[0], p, g), wi_v, p, *loads)
         put(act_v, p, g, a)
         put(h_v, p, g, (0.5 * a * (1.0 + jnp.tanh(GELU_C * (a + GELU_K * a * a * a)))).astype(BF16))
 
-    def forward_out(p, g):
-        rs_start(p, g, pair_dot(group(h_v, p, g), wo_v, p))
+    def forward_out(p, g, *loads):
+        rs_start(p, g, pair_dot(group(h_v, p, g), wo_v, p, *loads))
 
     NT = ((1,), (1,))
 
@@ -350,28 +371,26 @@
             dwi_v[e] = dot(group(recv_v.at[0], p, ALL) * mask, group(da_v, p, ALL), ((0,), (0,)))
 
     order = [(0, 0, OWN), (0, 0, MATE), (1, 0, NEAR), (2, 0, NEAR), (0, 1, FAR), (1, 1, FAR), (2, 1, FAR), (3, 0, NEAR), (3, 1, FAR)]
-    chunks = [(i, far, g[0] + b) for i, far, g in order for b in range(g[1])]
-
-    pieces = [(0, 0), (1, 0), (2, 0), (0, 1), (1, 1), (2, 1), (3, 0)]
+    chunks = [(i, far, g[0] + b, n) for i, far, g in order for b in range(g[1]) for n in (HALVES if i == LAST else range(1))]
+
+    pieces = [(0, 0), (1, 0), (2, 0), (0, 1), (1, 1), (2, 1)]
 
     def relay(at, k):
         with jax.named_scope(f"relay{at}_{k}"):
             if at == 3:
                 back_first(*pieces[k])
             else:
-                rs_relay(at, chunks[k][0], chunks[k][2])
+                rs_relay(at, *chunks[k])
 
     def wait_both(t, p):
         wait_rows(t, p, 0)
         wait_rows(t, p, 1)
 
     def own_act():
-        load_wi[0].wait()
-        forward_act(0, OWN)
+        forward_act(0, OWN, *load_wi[:2])
 
     def own_out():
-        load_wo[0].wait()
-        forward_out(0, OWN)
+        forward_out(0, OWN, *load_wo[:2])
 
     def start_mate():
         wait_rows(0, 0, 0)
@@ -379,12 +398,12 @@
         forward_out(0, MATE)
 
     def near_next():
-        load_wi[1].wait()
+        load_wi[2].wait()
         wait_rows(0, 1, 0)
         forward_act(1, NEAR)
 
     def near_next_out():
-        load_wo[1].wait()
+        load_wo[2].wait()
         forward_out(1, NEAR)
 
     def back_units(p, g, wait):
@@ -421,7 +440,8 @@
     work += timed(13.5, (0.42, 0.6, 0.42, 0.6), back_units(0, FAR, lambda: wait_rows(1, 0, 1)))
     work += timed(16.5, (0.47, 0.65, 0.47, 0.65), back_units(1, ALL, lambda: wait_both(1, 1)))
     work += timed(16.5, (0.61,) * 8, [functools.partial(weight_grad, n) for n in range(8)])
-    relays = [(7.0 + 1.33 * k, 1, k) for k in range(16)] + [(11.4 + 1.33 * k, 2, k) for k in range(16)]
+    when = [1.33 * (min(k, 12) + max(k - 12, 0) / 2) for k in range(20)]
+    relays = [(start + t, at, k) for start, at in ((7.0, 1), (11.4, 2)) for k, t in enumerate(when)]
     relays = sorted(relays + [(28.4 + 1.31 * k, 3, k) for k in range(3)])
     now, n_work = 7.2, 0
     while relays or work:
@@ -443,8 +463,8 @@
     def back(i, far):
         step("back2_", back_second, i, far)
 
-    for k in range(16):
-        step(f"final{k}_", rs_final, *chunks[k])
+    for k, chunk in enumerate(chunks):
+        step(f"final{k}", lambda: rs_final(*chunk))
         if k == 12:
             step("gate_root", gate_root)
     def finish_wg():
@@ -454,22 +474,24 @@
     def hand_over():
         back_v[...] = slots_v[...]
 
-    for n in range(2, 7):
+    blocks = [(far, b) for far in HALVES for b in HALVES]
+    for n in range(2, 6):
         if n > 2:
             turn(*pieces[n])
         back(*pieces[n - 2])
-        if n == 5:
-            step("router_back", router_back)
+    step("router_back", router_back)
+    back(*pieces[4])
+    step("last_first", last_first, *blocks[0])
+    step("last_first", last_first, *blocks[1])
     back(*pieces[5])
-    step("last_first", last_first, 0)
-    step("last_first", last_first, 1)
-    back(*pieces[6])
-    step("last_second", last_second, 0)
-    step("last_second", last_second, 1)
-    for n in range(7):
-        step("back3_", back_last, *pieces[n])
-    step("last_last", last_last, 0)
-    step("last_last", last_last, 1)
+    step("last_first", last_first, *blocks[2])
+    step("last_first", last_first, *blocks[3])
+    for far, b in blocks:
+        step("last_second", last_second, far, b)
+    for piece in pieces:
+        step("back3_", back_last, *piece)
+    for far, b in blocks:
+        step("last_last", last_last, far, b)
     step("hop_", hop_wait_end, 2)
     step("hop_", hop_wait_end, 3)
     step("hand_over", hand_over)
@@ -543,7 +565,7 @@
             pltpu.VMEM((4, 2, N_EP, block, half), F32), pltpu.VMEM((4, 2, N_EP, block, half), F32),
             pltpu.VMEM((4, N_EP, block, half), BF16), pltpu.VMEM((4, 2, N_EP, block, half), BF16),
             pltpu.VMEM((n_exp, d_model), F32), pltpu.VMEM((3, n_exp, d_model), F32), pltpu.VMEM((4, 8, n_tok), F32),
-            dma((8,)), dma((11,)), dma((2, 2, 2)), dma((4, 2, N_EP)), dma((4, 2)), dma((4, 2)), dma((4, 2)), dma((2, 2)), dma, dma((2,)),
+            dma((10,)), dma((11,)), dma((2, 2, 2)), dma((5, 2, N_EP)), dma((4, 2)), dma((3, 2)), dma((3, 2)), dma((2, 2, 2)), dma, dma((2,)),
         ]
         results = pl.pallas_call(
             functools.partial(moe_kernel, cap),

time: 57.1 us -> 56.9 us (level)
  no operation moved by 1% of the time
where the time goes in v6:
time: 56.9 us; the launch traced here: 56.7 us
  Pallas kernels  55.9 us (98%)
  between operations  0.8 us (1%)
    pallas_call x1, Pallas kernels, local_block(): pl.pallas_call(functools.partial(moe_kernel, cap), out_shape=held, in_spe...  49.2 us
    pallas_call x1, Pallas kernels, local_block(): pl.pallas_call(store_kernel, out_shape=out_shape, in_specs=[vmem_spec] *...  6.79 us

profile of v6, /device:TPU:0, one launch (start us, length us, event | category | flops | bytes accessed | tf_op | source)
XLA Modules:
  0.0 56.7 jit_solution(11287869852962774319)
XLA Ops:
  0.6 49.2 %shard_map.101 = (f32[256,128]{1,0:T(8,128)S(1)}, bf16[4,2,4,40,384]{4,3,2,1,0:T(8,128)(2,1)S(1)}, bf16[320,256]{1,0:T(8,128)(2,1)S(1)}, f32[256,768]{1,0:T(8,12...) custom-call(s32[1,256]{1,0:T(1,128)} %bitcast.4, bf16[16,768]{1,0:T(8,128)(2,1)} %bitcast.3, ...), custom_call_target="tpu_custom_call" | custom-call | tf_op jit(solution)/shard_map/pallas_call | solution.py:570
  49.8 6.8 %shard_map.102 = (bf16[256,768]{1,0:T(8,128)(2,1)}, bf16[256,768]{1,0:T(8,128)(2,1)}, f32[16,768]{1,0:T(8,128)}, f32[4,768,768]{2,1,0:T(8,128)}, f32[4,768,768]{2,1,0:T(8,128)}) custom-call(f32[256,128]{1,0:T(8,128)S(1)} %get-tuple-element.17.gate_v, bf16[4,2,4,40,384]{4,3,2,1,0:T(8,128)(2,1)S(1)} %get-tuple-element.18.back_v, ...), custom_call_target="tpu_custom_call" | custom-call | tf_op jit(solution)/shard_map/pallas_call | solution.py:581

commit v7 on v6

--- a/solution.py
+++ b/solution.py
@@ -40,12 +40,12 @@
 def moe_kernel(
     cap,
     ids_hbm, wg_hbm, x_hbm, gy_hbm, wi_hbm, wo_hbm,
-    gate_v, back_v, onehot_slots, rgrad_v, dwg_v, dwi_v, dwo_v,
+    gate_v, slots_v, onehot_slots, rgrad_v, dwg_v, dwi_v, dwo_v,
     ids_ref, wg_ref, x_v, gy_v, wi_v, wo_v,
     router_v, send_v, recv_v, act_v, h_v, da_v, tmp_v,
-    part_v, rs_in, red_v, slots_v,
+    part_v, rs_in, red_v,
     dwg_part, dwg_in, gate_rows,
-    load_sem, sent_sem, disp_recv, rs_recv, hop_recv, turn_recv, back_recv, last_recv, wg_recv, gate_recv,
+    load_sem, sent_sem, disp_recv, rs_recv, hop_recv, back_recv, last_recv, wg_recv, gate_recv,
 ):
     block = 2 * cap
     rows = N_EP * block
@@ -219,7 +219,7 @@
         return remote(2, red_v.at[i, q], slots_v.at[i, h, j], hop_recv.at[i, far], ep=q)
 
     def turn_copy(i, h, q, far):
-        return remote(5, red_v.at[i, q], slots_v.at[i, h, j], turn_recv.at[i, far], tp=behind[h], ep=q)
+        return remote(5, red_v.at[i, q], slots_v.at[i, h, j], hop_recv.at[i, far], tp=behind[h], ep=q)
 
     def last_turn(h, q, far):
         return remote(7, red_v.at[LAST, q], slots_v.at[LAST, h, j], last_recv.at[0, far, lax.rem(j, 2)], tp=behind[h], ep=q)
@@ -289,7 +289,7 @@
         for h in HALVES:
             @pl.when(place[h] == 2)
             def _():
-                wait_bytes(slots_v.at[i, h, pl.ds(0, 2)], turn_recv.at[i, far])
+                wait_bytes(slots_v.at[i, h, pl.ds(0, 2)], hop_recv.at[i, far])
                 back_copy(i, h, far).start()
 
     def back_second(i, far):
@@ -307,7 +307,7 @@
 
     def gate_copy(h, at):
         tp = at if h == 0 else N_TP - 1 - at
-        return remote(10, gate_rows.at[h], gate_rows.at[h], gate_recv.at[h], tp=tp)
+        return remote(6, gate_rows.at[h], gate_rows.at[h], gate_recv.at[h], tp=tp)
 
     def gate_root():
         for h in HALVES:
@@ -471,9 +471,6 @@
         wait_bytes(dwg_in, wg_recv)
         dwg_v[...] = (dwg_part[...] + dwg_in[0]) + (dwg_in[1] + dwg_in[2])
 
-    def hand_over():
-        back_v[...] = slots_v[...]
-
     blocks = [(far, b) for far in HALVES for b in HALVES]
     for n in range(2, 6):
         if n > 2:
@@ -494,7 +491,6 @@
         step("last_last", last_last, far, b)
     step("hop_", hop_wait_end, 2)
     step("hop_", hop_wait_end, 3)
-    step("hand_over", hand_over)
     step("finish_wg", finish_wg)
 
     def drain():
@@ -507,7 +503,7 @@
             wait_bytes(red_v.at[:, pl.ds(0, N_EP - 1)], sent_sem.at[2])
             wait_bytes(red_v.at[pl.ds(0, 3)], sent_sem.at[5])
             wait_bytes(red_v.at[0], sent_sem.at[7])
-            wait_bytes(gate_rows.at[pl.ds(0, 3)], sent_sem.at[10])
+            wait_bytes(gate_rows.at[pl.ds(0, 3)], sent_sem.at[6])
 
         @pl.when(jnp.logical_not(at_end))
         def _():
@@ -563,9 +559,9 @@
             pltpu.VMEM((2, N_EP, block, f_loc), F32), pltpu.VMEM((2, N_EP, block, f_loc), BF16),
             pltpu.VMEM((2, N_EP, block, f_loc), BF16), pltpu.VMEM((2, N_EP, block, d_model), F32),
             pltpu.VMEM((4, 2, N_EP, block, half), F32), pltpu.VMEM((4, 2, N_EP, block, half), F32),
-            pltpu.VMEM((4, N_EP, block, half), BF16), pltpu.VMEM((4, 2, N_EP, block, half), BF16),
+            pltpu.VMEM((4, N_EP, block, half), BF16),
             pltpu.VMEM((n_exp, d_model), F32), pltpu.VMEM((3, n_exp, d_model), F32), pltpu.VMEM((4, 8, n_tok), F32),
-            dma((10,)), dma((11,)), dma((2, 2, 2)), dma((5, 2, N_EP)), dma((4, 2)), dma((3, 2)), dma((3, 2)), dma((2, 2, 2)), dma, dma((2,)),
+            dma((10,)), dma((9,)), dma((2, 2, 2)), dma((5, 2, N_EP)), dma((4, 2)), dma((3, 2)), dma((2, 2, 2)), dma, dma((2,)),
         ]
         results = pl.pallas_call(
             functools.partial(moe_kernel, cap),

time: 56.9 us -> 56.7 us (level)
  no operation moved by 1% of the time
where the time goes in v7:
time: 56.7 us; the launch traced here: 56.6 us
  Pallas kernels  55.8 us (98%)
  between operations  0.8 us (1%)
    pallas_call x1, Pallas kernels, local_block(): pl.pallas_call(functools.partial(moe_kernel, cap), out_shape=held, in_spe...  49 us
    pallas_call x1, Pallas kernels, local_block(): pl.pallas_call(store_kernel, out_shape=out_shape, in_specs=[vmem_spec] *...  6.79 us

profile of v7, /device:TPU:0, one launch (start us, length us, event | category | flops | bytes accessed | tf_op | source)
XLA Modules:
  0.0 56.6 jit_solution(484800439445964750)
XLA Ops:
  0.6 49.0 %shard_map.101 = (f32[256,128]{1,0:T(8,128)S(1)}, bf16[4,2,4,40,384]{4,3,2,1,0:T(8,128)(2,1)S(1)}, bf16[320,256]{1,0:T(8,128)(2,1)S(1)}, f32[256,768]{1,0:T(8,12...) custom-call(s32[1,256]{1,0:T(1,128)} %bitcast.4, bf16[16,768]{1,0:T(8,128)(2,1)} %bitcast.3, ...), custom_call_target="tpu_custom_call" | custom-call | tf_op jit(solution)/shard_map/pallas_call | solution.py:566
  49.6 6.8 %shard_map.102 = (bf16[256,768]{1,0:T(8,128)(2,1)}, bf16[256,768]{1,0:T(8,128)(2,1)}, f32[16,768]{1,0:T(8,128)}, f32[4,768,768]{2,1,0:T(8,128)}, f32[4,768,768]{2,1,0:T(8,128)}) custom-call(f32[256,128]{1,0:T(8,128)S(1)} %get-tuple-element.17.gate_v, bf16[4,2,4,40,384]{4,3,2,1,0:T(8,128)(2,1)S(1)} %get-tuple-element.18.back_v, ...), custom_call_target="tpu_custom_call" | custom-call | tf_op jit(solution)/shard_map/pallas_call | solution.py:577

commit v8 on v7

--- a/solution.py
+++ b/solution.py
@@ -45,7 +45,7 @@
     router_v, send_v, recv_v, act_v, h_v, da_v, tmp_v,
     part_v, rs_in, red_v,
     dwg_part, dwg_in, gate_rows,
-    load_sem, sent_sem, disp_recv, rs_recv, hop_recv, back_recv, last_recv, wg_recv, gate_recv,
+    load_sem, sent_sem, disp_recv, rs_recv, hop_recv, last_recv, wg_recv, gate_recv,
 ):
     block = 2 * cap
     rows = N_EP * block
@@ -68,14 +68,14 @@
         pltpu.make_async_copy(ref, ref, sem).wait()
 
     load_x = pltpu.make_async_copy(x_hbm, x_v, load_sem.at[0])
-    load_gy = pltpu.make_async_copy(gy_hbm, gy_v, load_sem.at[1])
+    load_gy = pltpu.make_async_copy(gy_hbm, gy_v, load_sem.at[8])
     def load_weights(src, dst, first, count, n):
         return pltpu.make_async_copy(src.at[pl.ds(first, count)], dst.at[pl.ds(first, count)], load_sem.at[n])
 
-    load_wi = [load_weights(wi_hbm, wi_v, *a) for a in ((0, 1, 2), (1, 1, 3), (2, 2, 4))]
-    load_wo = [load_weights(wo_hbm, wo_v, *a) for a in ((0, 1, 8), (1, 1, 9), (2, 2, 5))]
-    load_ids = pltpu.make_async_copy(ids_hbm, ids_ref, load_sem.at[6])
-    load_wg = pltpu.make_async_copy(wg_hbm, wg_ref, load_sem.at[7])
+    load_wi = [load_weights(wi_hbm, wi_v, *a) for a in ((0, 1, 2), (1, 1, 3), (2, 2, 6))]
+    load_wo = [load_weights(wo_hbm, wo_v, *a) for a in ((0, 1, 4), (1, 1, 5), (2, 2, 7))]
+    load_ids = pltpu.make_async_copy(ids_hbm, ids_ref, load_sem.at[1])
+    load_wg = pltpu.make_async_copy(wg_hbm, wg_ref, load_sem.at[9])
     for load in (load_ids, load_x, *load_wi[:2], *load_wo[:2], load_wg, load_gy, load_wi[2], load_wo[2]):
         load.start()
 
@@ -283,7 +283,7 @@
 
     def back_copy(i, h, far):
         part = slots_v.at[i, h, pl.ds(side[far], 2)]
-        return remote(3, part, part, back_recv.at[i, far], tp=behind[h])
+        return remote(3, part, part, load_sem.at[2 * i + far], tp=behind[h])
 
     def back_first(i, far):
         for h in HALVES:
@@ -561,7 +561,7 @@
             pltpu.VMEM((4, 2, N_EP, block, half), F32), pltpu.VMEM((4, 2, N_EP, block, half), F32),
             pltpu.VMEM((4, N_EP, block, half), BF16),
             pltpu.VMEM((n_exp, d_model), F32), pltpu.VMEM((3, n_exp, d_model), F32), pltpu.VMEM((4, 8, n_tok), F32),
-            dma((10,)), dma((9,)), dma((2, 2, 2)), dma((5, 2, N_EP)), dma((4, 2)), dma((3, 2)), dma((2, 2, 2)), dma, dma((2,)),
+            dma((10,)), dma((9,)), dma((2, 2, 2)), dma((5, 2, N_EP)), dma((4, 2)), dma((2, 2, 2)), dma, dma((2,)),
         ]
         results = pl.pallas_call(
             functools.partial(moe_kernel, cap),

time: 56.7 us -> 56.7 us (level)
  no operation moved by 1% of the time
where the time goes in v8:
time: 56.7 us; the launch traced here: 56.5 us
  Pallas kernels  55.7 us (98%)
  between operations  0.8 us (1%)
    pallas_call x1, Pallas kernels, local_block(): pl.pallas_call(functools.partial(moe_kernel, cap), out_shape=held, in_spe...  48.9 us
    pallas_call x1, Pallas kernels, local_block(): pl.pallas_call(store_kernel, out_shape=out_shape, in_specs=[vmem_spec] *...  6.79 us

profile of v8, /device:TPU:0, one launch (start us, length us, event | category | flops | bytes accessed | tf_op | source)
XLA Modules:
  0.0 56.5 jit_solution(4745645166481323933)
XLA Ops:
  0.6 48.9 %shard_map.101 = (f32[256,128]{1,0:T(8,128)S(1)}, bf16[4,2,4,40,384]{4,3,2,1,0:T(8,128)(2,1)S(1)}, bf16[320,256]{1,0:T(8,128)(2,1)S(1)}, f32[256,768]{1,0:T(8,12...) custom-call(s32[1,256]{1,0:T(1,128)} %bitcast.4, bf16[16,768]{1,0:T(8,128)(2,1)} %bitcast.3, ...), custom_call_target="tpu_custom_call" | custom-call | tf_op jit(solution)/shard_map/pallas_call | solution.py:566
  49.6 6.8 %shard_map.102 = (bf16[256,768]{1,0:T(8,128)(2,1)}, bf16[256,768]{1,0:T(8,128)(2,1)}, f32[16,768]{1,0:T(8,128)}, f32[4,768,768]{2,1,0:T(8,128)}, f32[4,768,768]{2,1,0:T(8,128)}) custom-call(f32[256,128]{1,0:T(8,128)S(1)} %get-tuple-element.17.gate_v, bf16[4,2,4,40,384]{4,3,2,1,0:T(8,128)(2,1)S(1)} %get-tuple-element.18.back_v, ...), custom_call_target="tpu_custom_call" | custom-call | tf_op jit(solution)/shard_map/pallas_call | solution.py:577
